TPU v7x, 16 devices: a 4x2x1 block of a 4x4x8 slice. The times are simulated.
16 devices in a mesh: batch: 2 (over y, z), g: 8 (over x, core).
Axes of the slice: x: 4, y: 2, z: 1, core: 2. Of those that a mesh axis runs over, the one named last changes fastest.
The devices are a block of a 4x4x8 slice.
Arguments:
- keys: float32 [131072], P(('batch', 'g')), parts along dimension 0
- payload: bfloat16 [131072, 256], P(('batch', 'g')), parts along dimension 0
Outputs:
- output 1: float32 [262144], P(('batch', 'g')), parts along dimension 0
- output 2: bfloat16 [262144, 256], P(('batch', 'g')), parts along dimension 0
- output 3: int32 [16], P(('batch', 'g')), parts along dimension 0
There are 2 independent parts. A program takes and returns all parts, laid end to end along the dimension named above; each array names one.
All inputs are finite; a program needn't handle non-finite values.
Results may differ from a plain program's by a relative error of at most 0.001.
Values are sent between devices in bfloat16 or wider.
A program may use at most 768 MiB of HBM per device.

v0:
```python
import jax
import jax.numpy as jnp
from jax import lax
from jax.sharding import PartitionSpec as P

PAD_KEY = 128.0


def solution(mesh):
    group_size = mesh.shape["g"]

    def local_part(keys_loc, rows_loc):
        n_dev = keys_loc.shape[0]
        width = rows_loc.shape[1]
        cap_rows = 2 * n_dev // group_size
        sorted_keys, sort_order = lax.sort((keys_loc, lax.iota(jnp.int32, n_dev)), num_keys=1)
        samples = sorted_keys[:: n_dev // group_size]
        all_samples = jnp.sort(lax.all_gather(samples, "g", tiled=True))
        splitters = all_samples[group_size + group_size // 2 :: group_size]
        edges = jnp.searchsorted(sorted_keys, splitters, side="left").astype(jnp.int32)
        starts = jnp.concatenate([jnp.zeros((1,), jnp.int32), edges])
        stops = jnp.concatenate([edges, jnp.full((1,), n_dev, jnp.int32)])
        src_pos = starts[:, None] + lax.iota(jnp.int32, cap_rows)[None, :]
        is_valid = src_pos < stops[:, None]
        src_pos = jnp.minimum(src_pos, n_dev - 1)
        send_keys = jnp.where(is_valid, sorted_keys[src_pos], PAD_KEY)
        send_rows = jnp.where(is_valid[:, :, None], rows_loc[sort_order[src_pos]], 0.0)
        recv_keys = lax.all_to_all(send_keys, "g", 0, 0, tiled=True)
        recv_rows = lax.all_to_all(send_rows, "g", 0, 0, tiled=True)
        flat_keys = recv_keys.reshape(-1)
        merged_keys, merge_order = lax.sort((flat_keys, lax.iota(jnp.int32, flat_keys.shape[0])), num_keys=1)
        merged_rows = recv_rows.reshape(-1, width)[merge_order]
        own_count = jnp.sum(flat_keys < PAD_KEY).astype(jnp.int32).reshape(1)
        return merged_keys, merged_rows, own_count

    row_spec = P(("batch", "g"))
    mat_spec = P(("batch", "g"), None)
    return jax.shard_map(local_part, mesh=mesh, in_specs=(row_spec, mat_spec), out_specs=(row_spec, mat_spec, row_spec), check_vma=False)
```

profile of v0, /device:TPU:113, one launch (start us, length us, event | category | flops | bytes accessed | tf_op | source)
XLA Modules:
  0.0 460.9 jit_solution(11563012781184996902)
XLA Ops:
  0.7 7.1 %sort.45 = (f32[8192]{0:T(1024)S(1)}, s32[8192]{0:T(1024)S(1)}) sort(f32[8192]{0:T(1024)} %param.4, s32[8192]{0:T(1024)S(1)} %iota.22), dimensions={0}, to_apply=%region_0.0 | sort | flops 106496 | bytes 131072 | tf_op jit(solution)/shard_map/sort | solution.py:16
  7.8 0.1 slice.6
  7.9 1.2 dynamic-slice
  9.8 0.2 dynamic-update-slice
  10.1 13.5 %all-reduce = f32[64]{0:T(128)S(1)} all-reduce(f32[64]{0:T(128)S(1)} %dynamic-update-slice), channel_id=1, replica_groups=mesh['batch'=2,'g'=8] {'g'}, use_global_device_ids=true, to_apply=%add | all-reduce | flops 64 | bytes 512
  23.6 2.1 sort.46
  25.7 0.1 slice.7
  25.8 10.2 %while.24 = (s32[]{:T(128)}, u32[7]{0:T(128)S(1)}, u32[7]{0:T(128)S(1)}, f32[7]{0:T(128)S(1)}, pred[7]{0:T(512)(128)(4,1)S(1)}, /*index=5*/f32[8192]{0:T(1024)S(1)}, s32[]{:T(128)}, s32[]{:T(128)}, s32[]{}) while((s32[]{:T(128)}, u32[7]{0:T(128)S(1)}, u32[7]{0:T(128)S(1)}, f32[7]{0:T(128)S(1)}, pred[7]{0:T(512)(128)(4,1)S(1)}, ...), condition=%wide.region_3.4_spmd.clone, body=%wide.region_2.3_spmd.clone.sunk | while | flops 1259 | bytes 4710 | solution.py:20
  25.8 0.6 gather_fusion
  26.5 0.6 gather_fusion
  27.3 0.6 gather_fusion
  28.0 0.6 gather_fusion
  28.7 0.6 gather_fusion
  29.5 0.6 gather_fusion
  30.2 0.6 gather_fusion
  30.9 0.6 gather_fusion
  31.6 0.6 gather_fusion
  32.4 0.6 gather_fusion
  33.1 0.6 gather_fusion
  33.8 0.6 gather_fusion
  34.5 0.6 gather_fusion
  35.3 0.6 gather_fusion
  36.0 0.1 pad_add_fusion.1
  36.1 0.1 fusion.5
  36.2 90.5 %gather_fusion.1 = f32[16384]{0:T(1024)S(1)} fusion(f32[8192]{0:T(1024)S(1)} %get-tuple-element.191, s32[16384]{0:T(1024)S(1)} %broadcast_clamp_fusion.1), kind=kCustom, calls=%fused_computation.1 | custom fusion | bytes 196608 | tf_op jit(solution)/shard_map/gather | solution.py:26
  126.7 0.8 compare_select_fusion.5
  127.5 6.2 %all-to-all-start = ((f32[8,1,2048]{2,1,0:T(1,128)}), f32[8,1,2048]{2,1,0:T(1,128)S(1)}, u32[]{:S(2)}, u32[]{:S(2)}) async-start(f32[8,1,2048]{2,1,0:T(1,128)} %compare_select_fusion.5), calls=%async_computation | async-start | bytes 131072 | tf_op jit(solution)/shard_map/all_to_all | solution.py:28
  133.8 0.1 add_compare_fusion
  133.9 90.5 %gather_fusion.2 = s32[16384]{0:T(1024)S(1)} fusion(s32[8192]{0:T(1024)S(1)} %get-tuple-element.84, s32[16384]{0:T(1024)S(1)} %broadcast_clamp_fusion.1), kind=kCustom, calls=%fused_computation.2 | custom fusion | bytes 196608 | tf_op jit(solution)/shard_map/gather | solution.py:27
  224.5 64.0 %gather_fusion.3 = bf16[16384,256]{1,0:T(8,128)(2,1)} fusion(bf16[8192,256]{1,0:T(8,128)(2,1)} %param.5, s32[16384]{0:T(1024)S(1)} %broadcast_clamp_fusion), kind=kCustom, calls=%fused_computation.3 | custom fusion | bytes 16842752 | tf_op jit(solution)/shard_map/gather | solution.py:27
  288.5 8.0 %broadcast_select_fusion.2 = bf16[8,2048,256]{2,1,0:T(8,128)(2,1)} fusion(bf16[8,2048,256]{2,1,0:T(8,128)(2,1)} %bitcast.14, pred[8,2048]{1,0:T(8,128)(4,1)S(1)} %add_compare_fusion), kind=kLoop, calls=%fused_computation.19 | loop fusion | flops 4194304 | bytes 16793600 | tf_op jit(solution)/shard_map/jit(_where)/select_n | solution.py:27
  296.5 0.0 all-to-all-done
  296.5 5.2 %all-to-all-start.1 = ((bf16[8,2048,256]{2,1,0:T(8,128)(2,1)}), bf16[8,2048,256]{2,1,0:T(8,128)(2,1)}, u32[]{:S(2)}, u32[]{:S(2)}) async-start(bf16[8,2048,256]{2,1,0:T(8,128)(2,1)} %broadcast_select_fusion.2), calls=%async_computation.1 | async-start | bytes 16777216 | tf_op jit(solution)/shard_map/all_to_all | solution.py:29
  301.8 8.7 %sort.47 = (f32[16384]{0:T(1024)}, s32[16384]{0:T(1024)S(1)}) sort(f32[16384]{0:T(1024)S(1)} %bitcast.15, s32[16384]{0:T(1024)S(1)} %iota.24), dimensions={0}, to_apply=%region_4.5 | sort | flops 229376 | bytes 262144 | tf_op jit(solution)/shard_map/sort | solution.py:31
  310.5 0.1 broadcast_compare_fusion
  310.6 0.7 convert_reduce_fusion
  311.2 84.0 %all-to-all-done.1 = bf16[8,2048,256]{2,1,0:T(8,128)(2,1)} async-done(((bf16[8,2048,256]{2,1,0:T(8,128)(2,1)}), bf16[8,2048,256]{2,1,0:T(8,128)(2,1)}, u32[]{:S(2)}, u32[]{:S(2)}) %all-to-all-start.1) | async-done | bytes 8388640 | tf_op jit(solution)/shard_map/all_to_all | solution.py:29
  395.2 65.7 %gather_fusion.4 = bf16[16384,256]{1,0:T(8,128)(2,1)} fusion(bf16[16384,256]{1,0:T(8,128)(2,1)} %bitcast.4, s32[16384]{0:T(1024)S(1)} %fusion.7), kind=kCustom, calls=%fused_computation.4 | custom fusion | bytes 16842752 | tf_op jit(solution)/shard_map/gather | solution.py:32
  (85 shorter events, 0.7 us)
Async XLA Ops:
  127.5 169.0 %all-to-all-start = ((f32[8,1,2048]{2,1,0:T(1,128)}), f32[8,1,2048]{2,1,0:T(1,128)S(1)}, u32[]{:S(2)}, u32[]{:S(2)}) async-start(f32[8,1,2048]{2,1,0:T(1,128)} %compare_select_fusion.5), calls=%async_computation | async-start | bytes 131072 | tf_op jit(solution)/shard_map/all_to_all | solution.py:28
  296.5 98.8 %all-to-all-start.1 = ((bf16[8,2048,256]{2,1,0:T(8,128)(2,1)}), bf16[8,2048,256]{2,1,0:T(8,128)(2,1)}, u32[]{:S(2)}, u32[]{:S(2)}) async-start(bf16[8,2048,256]{2,1,0:T(8,128)(2,1)} %broadcast_select_fusion.2), calls=%async_computation.1 | async-start | bytes 16777216 | tf_op jit(solution)/shard_map/all_to_all | solution.py:29
where the time goes:
time: 462 us; the launch traced here: 461 us
  local copies, waits for them, and re-layouts  321 us (69%)
  waiting for transfers between devices  84 us (18%)
  other arithmetic  28.4 us (6%)
  blocking collectives  13.5 us (3%)
  starting transfers between devices  11.5 us (2%)
    gather x2, local copies, waits for them, and re-layouts, local_part(): sort_order[src_pos]  90.6 us
    gather x1, local copies, waits for them, and re-layouts, local_part(): send_keys = jnp.where(is_valid, sorted_keys[src_pos], PAD_KEY)  90.5 us
    all_to_all x1, waiting for transfers between devices, local_part(): recv_rows = lax.all_to_all(send_rows, 'g', 0, 0, tiled=True)  84 us
    gather x1, local copies, waits for them, and re-layouts, local_part(): merged_rows = recv_rows.reshape(-1, width)[merge_order]  65.7 us
    gather x1, local copies, waits for them, and re-layouts, local_part(): rows_loc[sort_order[src_pos]]  64 us
    unnamed x1, blocking collectives  13.5 us
  transfers between devices with their start and end apart: 2, of which 1 were waited for; matrix products, arithmetic and copies ran while one was open for 37% of the time, Pallas kernels for 0%

commit v1 on v0

v1 whole, which is shorter than its diff:
```python
import jax
import jax.numpy as jnp
from jax import lax
from jax.sharding import PartitionSpec as P

PAD_KEY = 128.0


def solution(mesh):
    group = mesh.shape["g"]

    def local_part(keys_loc, rows_loc):
        n = keys_loc.shape[0]
        width = rows_loc.shape[1]
        cap = 2 * n // group
        me = lax.axis_index("g")
        sorted_keys, order = lax.sort((keys_loc, lax.iota(jnp.int32, n)), num_keys=1)
        all_keys = lax.all_gather(sorted_keys, "g")
        samples = all_keys[:, :: n // group].reshape(-1)
        ranks = jnp.sum(samples[None, :] < samples[:, None], axis=1)
        want = group + group // 2 + group * lax.iota(jnp.int32, group - 1)
        splitters = jnp.sum(jnp.where(ranks[None, :] == want[:, None], samples[None, :], 0.0), axis=1)
        edges = jnp.sum(all_keys[:, None, :] < splitters[None, :, None], axis=-1).astype(jnp.int32)
        starts = jnp.concatenate([jnp.zeros((group, 1), jnp.int32), edges], axis=1)
        stops = jnp.concatenate([edges, jnp.full((group, 1), n, jnp.int32)], axis=1)
        counts = stops - starts
        slot = lax.iota(jnp.int32, cap)
        order_pad = jnp.concatenate([order, jnp.zeros((cap,), jnp.int32)])
        my_starts = lax.dynamic_index_in_dim(starts, me, 0, keepdims=False)
        send_idx = jnp.concatenate([lax.dynamic_slice(order_pad, (my_starts[d],), (cap,)) for d in range(group)])
        send_rows = rows_loc[send_idx].reshape(group, cap, width)
        recv_rows = lax.all_to_all(send_rows, "g", 0, 0, tiled=True)
        in_starts = lax.dynamic_index_in_dim(starts, me, 1, keepdims=False)
        in_counts = lax.dynamic_index_in_dim(counts, me, 1, keepdims=False)
        key_pad = jnp.concatenate([all_keys, jnp.full((group, cap), PAD_KEY)], axis=1)
        wins = []
        for s in range(group):
            win = lax.dynamic_slice(key_pad[s], (in_starts[s],), (cap,))
            wins.append(jnp.where(slot < in_counts[s], win, PAD_KEY))
        merged_keys, merge_order = lax.sort((jnp.concatenate(wins), lax.iota(jnp.int32, 2 * n)), num_keys=1)
        own = jnp.sum(in_counts)
        merged_rows = recv_rows.reshape(-1, width)[merge_order]
        merged_rows = jnp.where((lax.iota(jnp.int32, 2 * n) < own)[:, None], merged_rows, 0.0)
        return merged_keys, merged_rows, own.reshape(1)

    row_spec = P(("batch", "g"))
    mat_spec = P(("batch", "g"), None)
    return jax.shard_map(local_part, mesh=mesh, in_specs=(row_spec, mat_spec), out_specs=(row_spec, mat_spec, row_spec), check_vma=False)
```

time: 462 us -> 288 us (0.62)
  local copies, waits for them, and re-layouts: 321 us -> 133 us
  between operations: 1.44 us -> 30.7 us
  waiting for transfers between devices: 84 us -> 61.9 us
  blocking collectives: 13.5 us -> 19.2 us
    gather x18 -> x1, local copies, waits for them, and re-layouts: 254 us -> 64 us  [local_part(): send_rows = rows_loc[send_idx].reshape(group, cap, width)]
    all_to_all x1, waiting for transfers between devices: 84 us -> 61.9 us  [local_part(): recv_rows = lax.all_to_all(send_rows, 'g', 0, 0, tiled=True)]
    all_gather x0 -> x1, blocking collectives: none -> 19.2 us  [local_part(): all_keys = lax.all_gather(sorted_keys, 'g')]
    unnamed x1 -> x0, blocking collectives: 13.5 us -> none
    all_to_all x1 -> x0, starting transfers between devices: 6.25 us -> none  [local_part(): recv_keys = lax.all_to_all(send_keys, 'g', 0, 0, tiled=True)]
    all_to_all x1, starting transfers between devices: 5.25 us -> 11 us  [local_part(): recv_rows = lax.all_to_all(send_rows, 'g', 0, 0, tiled=True)]
    sort x3 -> x2, other arithmetic: 18 us -> 15.9 us  [the longest x1 8.73 us: local_part(): lax.sort((jnp.concatenate(wins), lax.iota(jnp.int32, 2 * n)), num_keys=1)]
  transfers between devices with their start and end apart: 2 -> 1, of which waited for: 1 -> 1; matrix products, arithmetic and copies ran while one was open for 37% -> 6% of each run, Pallas kernels for 0% -> 0%
where the time goes in v1:
time: 288 us; the launch traced here: 286 us
  local copies, waits for them, and re-layouts  133 us (46%)
  waiting for transfers between devices  61.9 us (21%)
  other arithmetic  31 us (11%)
  between operations  30.7 us (11%)
  blocking collectives  19.2 us (7%)
  starting transfers between devices  11 us (4%)
    gather x1, local copies, waits for them, and re-layouts, local_part(): merged_rows = recv_rows.reshape(-1, width)[merge_order]  65.7 us
    gather x1, local copies, waits for them, and re-layouts, local_part(): send_rows = rows_loc[send_idx].reshape(group, cap, width)  64 us
    all_to_all x1, waiting for transfers between devices, local_part(): recv_rows = lax.all_to_all(send_rows, 'g', 0, 0, tiled=True)  61.9 us
    all_gather x1, blocking collectives, local_part(): all_keys = lax.all_gather(sorted_keys, 'g')  19.2 us
    all_to_all x1, starting transfers between devices, local_part(): recv_rows = lax.all_to_all(send_rows, 'g', 0, 0, tiled=True)  11 us
    sort x1, other arithmetic, local_part(): lax.sort((jnp.concatenate(wins), lax.iota(jnp.int32, 2 * n)), num_keys=1)  8.73 us
    select_n x1, other arithmetic, local_part(): jnp.where((lax.iota(jnp.int32, 2 * n) < own)[:, None], merged_rows, 0.0)  8 us
    sort x1, other arithmetic, local_part(): lax.sort((keys_loc, lax.iota(jnp.int32, n)), num_keys=1)  7.14 us
  transfers between devices with their start and end apart: 1, of which 1 were waited for; matrix products, arithmetic and copies ran while one was open for 6% of the time, Pallas kernels for 0%

profile of v1, /device:TPU:113, one launch (start us, length us, event | category | flops | bytes accessed | tf_op | source)
XLA Modules:
  0.0 286.4 jit_solution(12901063292960153499)
XLA Ops:
  0.7 7.1 %sort.30 = (f32[8192]{0:T(1024)S(1)}, s32[8192]{0:T(1024)S(1)}) sort(f32[8192]{0:T(1024)} %param.2, s32[8192]{0:T(1024)S(1)} %iota.34), dimensions={0}, to_apply=%region_0.0 | sort | flops 106496 | bytes 131072 | tf_op jit(solution)/shard_map/sort | solution.py:17
  7.8 19.2 %all-gather = f32[65536]{0:T(1024)S(1)} all-gather(f32[8192]{0:T(1024)S(1)} %get-tuple-element.7), channel_id=2, replica_groups=mesh['batch'=2,'g'=8] {'g'}, dimensions={0}, use_global_device_ids=true | all-gather | bytes 294912 | tf_op jit(solution)/shard_map/all_gather | solution.py:18
  27.0 0.1 reshape.409
  27.0 0.1 slice.123
  27.1 0.1 lt.155
  27.2 0.2 convert_reduce_fusion.1
  27.4 0.2 select_reduce_fusion
  27.6 0.4 convert_reduce_fusion
  28.0 0.1 pad_dynamic-slice_fusion.8
  28.1 0.6 fusion.2
  43.9 0.1 pad_dynamic-slice_fusion
  44.1 0.1 compare_select_fusion
  44.2 64.0 %gather_fusion = bf16[16384,256]{1,0:T(8,128)(2,1)} fusion(bf16[8192,256]{1,0:T(8,128)(2,1)} %param.3, s32[16384]{0:T(1024)S(1)} %broadcast_clamp_fusion), kind=kCustom, calls=%fused_computation | custom fusion | bytes 16842752 | tf_op jit(solution)/shard_map/gather | solution.py:31
  108.2 11.0 %all-to-all-start = ((bf16[8,2048,256]{2,1,0:T(8,128)(2,1)}), bf16[8,2048,256]{2,1,0:T(8,128)(2,1)}, u32[]{:S(2)}, u32[]{:S(2)}) async-start(bf16[8,2048,256]{2,1,0:T(8,128)(2,1)} %bitcast.44), calls=%async_computation | async-start | bytes 16777216 | tf_op jit(solution)/shard_map/all_to_all | solution.py:32
  119.1 0.6 fusion.4
  134.5 0.6 fusion.1
  135.1 0.7 fusion.3
  135.8 0.2 pad_slice_fusion
  136.0 0.1 constant_dynamic-slice_fusion.6
  136.1 0.6 constant_dynamic-update-slice_fusion
  136.8 0.7 select_dynamic-update-slice_fusion.6
  137.4 0.1 constant_dynamic-slice_fusion.4
  137.5 0.6 select_dynamic-update-slice_fusion.5
  138.1 0.6 select_dynamic-update-slice_fusion.4
  138.7 0.1 constant_dynamic-slice_fusion.2
  138.8 0.6 select_dynamic-update-slice_fusion.3
  139.4 0.6 select_dynamic-update-slice_fusion.2
  140.1 0.1 constant_dynamic-slice_fusion
  140.2 0.6 select_dynamic-update-slice_fusion.1
  140.8 0.7 select_dynamic-update-slice_fusion
  141.4 8.7 %sort.31 = (f32[16384]{0:T(1024)}, s32[16384]{0:T(1024)S(1)}) sort(f32[16384]{0:T(1024)S(1)} %select_dynamic-update-slice_fusion, s32[16384]{0:T(1024)S(1)} %iota.43), dimensions={0}, to_apply=%region_4.5 | sort | flops 229376 | bytes 262144 | tf_op jit(solution)/shard_map/sort | solution.py:40
  150.2 0.7 iota_compare_fusion
  150.9 61.9 %all-to-all-done = bf16[8,2048,256]{2,1,0:T(8,128)(2,1)} async-done(((bf16[8,2048,256]{2,1,0:T(8,128)(2,1)}), bf16[8,2048,256]{2,1,0:T(8,128)(2,1)}, u32[]{:S(2)}, u32[]{:S(2)}) %all-to-all-start) | async-done | bytes 8388640 | tf_op jit(solution)/shard_map/all_to_all | solution.py:32
  212.7 65.7 %gather_fusion.1 = bf16[16384,256]{1,0:T(8,128)(2,1)} fusion(bf16[16384,256]{1,0:T(8,128)(2,1)} %bitcast.42, s32[16384]{0:T(1024)S(1)} %fusion), kind=kCustom, calls=%fused_computation.1 | custom fusion | bytes 16842752 | tf_op jit(solution)/shard_map/gather | solution.py:42
  278.4 8.0 %broadcast_select_fusion = bf16[16384,256]{1,0:T(8,128)(2,1)} fusion(bf16[16384,256]{1,0:T(8,128)(2,1)} %gather_fusion.1, pred[16384]{0:T(1024)(128)(4,1)S(1)} %iota_compare_fusion), kind=kLoop, calls=%fused_computation.2 | loop fusion | flops 4194304 | bytes 16793600 | tf_op jit(solution)/shard_map/jit(_where)/select_n | solution.py:43
  (15 shorter events, 0.1 us)
Async XLA Ops:
  108.2 104.6 %all-to-all-start = ((bf16[8,2048,256]{2,1,0:T(8,128)(2,1)}), bf16[8,2048,256]{2,1,0:T(8,128)(2,1)}, u32[]{:S(2)}, u32[]{:S(2)}) async-start(bf16[8,2048,256]{2,1,0:T(8,128)(2,1)} %bitcast.44), calls=%async_computation | async-start | bytes 16777216 | tf_op jit(solution)/shard_map/all_to_all | solution.py:32

commit v2 on v0

v2 whole, which is shorter than its diff:
```python
import functools

import jax
import jax.numpy as jnp
from jax import lax
from jax.experimental import pallas as pl
from jax.experimental.pallas import tpu as pltpu
from jax.sharding import PartitionSpec as P

PAD_KEY = 128.0
LANES = 128
MESH = pl.DeviceIdType.MESH


def greet(group):
    me = lax.axis_index("g")
    barrier = pltpu.get_barrier_semaphore()
    for off in range(1, group):
        pl.semaphore_signal(barrier, inc=1, device_id={"g": lax.rem(me + off, group)}, device_id_type=MESH)
    pl.semaphore_wait(barrier, group - 1)
    return me


def lane_prefix(x, lane):
    for step in (1, 2, 4):
        x = x + jnp.where(lane >= step, pltpu.roll(x, step, 1), 0)
    return x


def sub_prefix(x, sub):
    for step in (1, 2, 4):
        x = x + jnp.where(sub >= step, pltpu.roll(x, step, 0), 0)
    return x


def plan_kernel(group, n, cap, relay, keys_ref, rows_ref,
                win_ref, loc_ref, rows3_ref, tab_ref, idx1_ref, idx2_ref, info_ref,
                all_keys, tab_smem, send_sem, recv_sem, tab_sem):
    run_rows = n // LANES
    win_rows = 2 * run_rows // group
    me = greet(group)
    copies = []
    for off in range(1, group):
        copy = pltpu.make_async_remote_copy(
            src_ref=keys_ref, dst_ref=all_keys.at[me, pl.ds(0, run_rows)], send_sem=send_sem.at[off],
            recv_sem=recv_sem.at[off], device_id={"g": lax.rem(me + off, group)}, device_id_type=MESH)
        copy.start()
        copies.append(copy)
    all_keys[me, pl.ds(0, run_rows)] = keys_ref[...]
    tail = all_keys.shape[1] - run_rows
    for s in range(group):
        all_keys[s, pl.ds(run_rows, tail)] = jnp.full((tail, LANES), PAD_KEY, jnp.float32)

    def relayout(t, c):
        at = pl.multiple_of(t * 64, 64)
        rows3_ref[pl.ds(at, 64)] = rows_ref[pl.ds(at, 64)].reshape(64, 2, LANES)
        return c

    lax.fori_loop(0, n // 64, relayout, 0)
    for copy in copies:
        copy.wait()

    count = group * group
    stride = run_rows // group
    col = jnp.concatenate(
        [jnp.concatenate([all_keys[s, pl.ds(m * stride, 1)] for m in range(group)], axis=0) for s in range(group)], axis=0)
    col = jnp.broadcast_to(col[:, 0:1], (count, LANES))
    r_id = lax.broadcasted_iota(jnp.int32, (count, LANES), 0)
    l_id = lax.broadcasted_iota(jnp.int32, (count, LANES), 1)
    row = jnp.sum(jnp.where(r_id == l_id, col, 0.0), axis=0, keepdims=True)
    less = (jnp.broadcast_to(row, (count, LANES)) < col) & (l_id < count)
    rank = jnp.sum(jnp.where(less, 1.0, 0.0), axis=1, keepdims=True)
    want = (group * l_id + group // 2).astype(jnp.float32)
    splitters = jnp.sum(jnp.where(jnp.broadcast_to(rank, (count, LANES)) == want, col, 0.0), axis=0, keepdims=True)

    lane = lax.broadcasted_iota(jnp.int32, (group, LANES), 1)
    sub = lax.broadcasted_iota(jnp.int32, (group, LANES), 0)
    edges = jnp.where(lane < group, 0, n)
    for j in range(1, group):
        part = []
        for s in range(group):
            hit = jnp.where(all_keys[s, pl.ds(0, run_rows)] < splitters[0, j], 1, 0)
            part.append(jnp.sum(hit, axis=0, keepdims=True))
        total = jnp.sum(jnp.concatenate(part, axis=0), axis=1, keepdims=True)
        edges = jnp.where(lane == j, jnp.broadcast_to(total, (group, LANES)), edges)
    counts = jnp.where(lane < group, pltpu.roll(edges, LANES - 1, 1) - edges, 0)
    over = jnp.maximum(counts - cap, 0)
    share = jnp.right_shift(over + (group - 1), group.bit_length() - 1)
    first = lane_prefix(share, lane) - share
    second = sub_prefix(share, sub) - share
    worst = jnp.maximum(jnp.max(first + share), jnp.max(second + share))
    tab_ref[0] = edges
    tab_ref[1] = counts
    tab_ref[2] = share
    tab_ref[3] = first
    tab_ref[4] = second
    to_smem = pltpu.make_async_copy(tab_ref, tab_smem, tab_sem)
    to_smem.start()
    to_smem.wait()

    idx1 = jnp.zeros((group, LANES), jnp.int32)
    for j in range(group):
        q, a = tab_smem[2, me, j], tab_smem[3, me, j]
        src = tab_smem[0, me, j] + cap - a + q * sub + lane
        idx1 = jnp.where((lane >= a) & (lane < a + q), src, idx1)
    idx1_ref[...] = jnp.clip(idx1, 0, n - 1)
    lane1 = lane[0:1]
    for j in range(group):
        line = jnp.zeros((1, LANES), jnp.int32)
        for s in range(group):
            q, a, b = tab_smem[2, s, j], tab_smem[3, s, j], tab_smem[4, s, j]
            line = jnp.where((lane1 >= b) & (lane1 < b + q), s * relay + a - b + lane1, line)
        idx2_ref[pl.ds(j, 1)] = jnp.clip(line, 0, group * relay - 1)

    wl = lax.broadcasted_iota(jnp.int32, (win_rows, LANES), 1)
    pos = lax.broadcasted_iota(jnp.int32, (win_rows, LANES), 0) * LANES + wl
    own = jnp.int32(0)
    for s in range(group):
        start, num = tab_smem[0, s, me], tab_smem[1, s, me]
        q, b = tab_smem[2, s, me], tab_smem[4, s, me]
        own = own + num
        shift = jnp.bitwise_and(start, LANES - 1)
        at = jnp.right_shift(start, LANES.bit_length() - 1)
        turn = jnp.bitwise_and(LANES - shift, LANES - 1)
        one = pltpu.roll(all_keys[s, pl.ds(at, win_rows)], turn, 1)
        two = pltpu.roll(all_keys[s, pl.ds(at + 1, win_rows)], turn, 1)
        window = jnp.where(wl < LANES - shift, one, two)
        win_ref[pl.ds(s * win_rows, win_rows)] = jnp.where(pos < num, window, PAD_KEY)
        extra = pos - cap
        far = group * cap + b + extra
        for m in range(1, group):
            far = far + jnp.where(extra >= m * q, relay - q, 0)
        loc = jnp.where(pos < cap, s * cap + pos, far)
        loc_ref[pl.ds(s * win_rows, win_rows)] = jnp.where(pos < num, jnp.clip(loc, 0, group * (cap + relay) - 1), 0)
    info_ref[0] = own
    info_ref[1] = jnp.where(worst <= relay, 1, 0)


def exchange_kernel(group, cap, relay, unroll, order_ref, start_ref, idx1_ref, idx2_ref, rows_ref,
                    out_ref, near, far1, far2, got, near_sems, far1_sems, far2_sems):
    me = greet(group)

    def gather(dst, base, size, pick):
        def step(t, c):
            for u in range(unroll):
                r = t * unroll + u
                dst[base + r] = pick(r)
            return c
        lax.fori_loop(0, size // unroll, step, 0)

    def send(src, dst, sems, off):
        copy = pltpu.make_async_remote_copy(
            src_ref=src, dst_ref=dst, send_sem=sems.at[0, off], recv_sem=sems.at[1, off],
            device_id={"g": lax.rem(me + off, group)}, device_id_type=MESH)
        copy.start()
        return copy

    offsets = [2, 6, 4, 3, 7, 5, 1]
    firsts, others = [], []
    for off in offsets + [0]:
        peer = lax.rem(me + off, group)
        pick = lambda r: rows_ref[order_ref[idx1_ref[peer, r]]]
        if off:
            gather(far1.at[off], 0, relay, pick)
            firsts.append(send(far1.at[off], got.at[pl.ds(me * relay, relay)], far1_sems, off))
        else:
            gather(got, me * relay, relay, pick)
    for off in offsets + [0]:
        start = start_ref[lax.rem(me + off, group)]
        pick = lambda r: rows_ref[order_ref[start + r]]
        if off:
            gather(near.at[off], 0, cap, pick)
            others.append(send(near.at[off], out_ref.at[pl.ds(me * cap, cap)], near_sems, off))
        else:
            gather(out_ref, me * cap, cap, pick)
    for copy in firsts:
        copy.wait()
    base2 = group * cap + me * relay
    for off in offsets + [0]:
        peer = lax.rem(me + off, group)
        pick = lambda r: got[idx2_ref[peer, r]]
        if off:
            gather(far2.at[off], 0, relay, pick)
            others.append(send(far2.at[off], out_ref.at[pl.ds(base2, relay)], far2_sems, off))
        else:
            gather(out_ref, base2, relay, pick)
    for copy in others:
        copy.wait()


def place_kernel(block, unroll, loc_ref, info_ref, rows_ref, out_ref, tmp):
    base = pl.program_id(0) * block
    num = jnp.clip(info_ref[0] - base, 0, block)
    width = out_ref.shape[1]

    def step(t, c):
        for u in range(unroll):
            r = t * unroll + u
            tmp[r] = rows_ref[loc_ref[base + r]]
        return c

    lax.fori_loop(0, (num + unroll - 1) // unroll, step, 0)

    def finish(t, c):
        at = pl.multiple_of(t * 64, 64)
        x = tmp[pl.ds(at, 64)].reshape(64, width)
        row = at + lax.broadcasted_iota(jnp.int32, (64, width), 0)
        out_ref[pl.ds(at, 64)] = jnp.where(row < num, x, jnp.zeros_like(x))
        return c

    full = (num + 63) // 64
    lax.fori_loop(0, full, finish, 0)

    def blank(t, c):
        at = pl.multiple_of(t * 64, 64)
        out_ref[pl.ds(at, 64)] = jnp.zeros((64, width), out_ref.dtype)
        return c

    lax.fori_loop(full, block // 64, blank, 0)


def solution(mesh):
    group = mesh.shape["g"]

    def local_part(keys_loc, rows_loc):
        n = keys_loc.shape[0]
        width = rows_loc.shape[1]
        full_cap = 2 * n // group
        cap = n // group + n // group // 64
        relay = LANES
        total = group * (cap + relay)
        vmem, smem, hbm = pltpu.VMEM, pltpu.SMEM, pl.ANY
        spec = lambda m: pl.BlockSpec(memory_space=m)
        me = lax.axis_index("g")
        run_rows = n // LANES

        sorted_keys, order = lax.sort((keys_loc, lax.iota(jnp.int32, n)), num_keys=1)
        windows, locs, rows3, table, idx1, idx2, info = pl.pallas_call(
            functools.partial(plan_kernel, group, n, cap, relay),
            out_shape=[
                jax.ShapeDtypeStruct((2 * run_rows, LANES), jnp.float32),
                jax.ShapeDtypeStruct((2 * run_rows, LANES), jnp.int32),
                jax.ShapeDtypeStruct((n, 2, LANES), rows_loc.dtype),
                jax.ShapeDtypeStruct((5, group, LANES), jnp.int32),
                jax.ShapeDtypeStruct((group, LANES), jnp.int32),
                jax.ShapeDtypeStruct((group, LANES), jnp.int32),
                jax.ShapeDtypeStruct((2,), jnp.int32),
            ],
            in_specs=[spec(vmem), spec(vmem)],
            out_specs=[spec(vmem)] * 6 + [spec(smem)],
            scratch_shapes=[
                pltpu.VMEM((group, run_rows + 24, LANES), jnp.float32),
                pltpu.SMEM((5, group, LANES), jnp.int32),
                pltpu.SemaphoreType.DMA((group,)),
                pltpu.SemaphoreType.DMA((group,)),
                pltpu.SemaphoreType.DMA,
            ],
            compiler_params=pltpu.CompilerParams(collective_id=0, has_side_effects=True, vmem_limit_bytes=40 << 20),
            name="plan",
        )(sorted_keys.reshape(run_rows, LANES), rows_loc)

        merged_keys, merged_loc = lax.sort((windows.reshape(-1), locs.reshape(-1)), num_keys=1)
        my_starts = lax.dynamic_index_in_dim(table[0], me, 0, keepdims=False)
        order_pad = jnp.concatenate([order, jnp.zeros((full_cap,), jnp.int32)])
        recv = pl.pallas_call(
            functools.partial(exchange_kernel, group, cap, relay, 16),
            out_shape=jax.ShapeDtypeStruct((total, 2, LANES), rows_loc.dtype),
            in_specs=[spec(smem)] * 4 + [spec(vmem)],
            out_specs=spec(vmem),
            scratch_shapes=[
                pltpu.VMEM((group, cap, 2, LANES), rows_loc.dtype),
                pltpu.VMEM((group, relay, 2, LANES), rows_loc.dtype),
                pltpu.VMEM((group, relay, 2, LANES), rows_loc.dtype),
                pltpu.VMEM((group * relay, 2, LANES), rows_loc.dtype),
                pltpu.SemaphoreType.DMA((2, group)),
                pltpu.SemaphoreType.DMA((2, group)),
                pltpu.SemaphoreType.DMA((2, group)),
            ],
            compiler_params=pltpu.CompilerParams(collective_id=1, has_side_effects=True, vmem_limit_bytes=40 << 20),
            name="exchange",
        )(order_pad, my_starts, idx1, idx2, rows3)

        block = 1024

        def placed(recv, merged_loc):
            return pl.pallas_call(
                functools.partial(place_kernel, block, 32),
                grid_spec=pltpu.PrefetchScalarGridSpec(
                    num_scalar_prefetch=2,
                    grid=(2 * n // block,),
                    in_specs=[spec(vmem)],
                    out_specs=pl.BlockSpec((block, width), lambda i, *_: (i, 0)),
                    scratch_shapes=[pltpu.VMEM((block, 2, LANES), rows_loc.dtype)],
                ),
                out_shape=jax.ShapeDtypeStruct((2 * n, width), rows_loc.dtype),
                compiler_params=pltpu.CompilerParams(vmem_limit_bytes=40 << 20),
                name="place",
            )(merged_loc, info, recv)

        def padded(recv, merged_loc):
            send_idx = jnp.concatenate([lax.dynamic_slice(order_pad, (my_starts[d],), (full_cap,)) for d in range(group)])
            send_rows = rows_loc[send_idx].reshape(group, full_cap, width)
            recv_rows = lax.all_to_all(send_rows, "g", 0, 0, tiled=True)
            slots = lax.iota(jnp.int32, 2 * n)
            _, merge_order = lax.sort((windows.reshape(-1), slots), num_keys=1)
            rows = recv_rows.reshape(-1, width)[merge_order]
            return jnp.where((slots < info[0])[:, None], rows, 0.0)

        merged_rows = lax.cond(info[1] == 1, placed, padded, recv, merged_loc)
        return merged_keys, merged_rows, info[0:1]

    row_spec = P(("batch", "g"))
    mat_spec = P(("batch", "g"), None)
    return jax.shard_map(local_part, mesh=mesh, in_specs=(row_spec, mat_spec), out_specs=(row_spec, mat_spec, row_spec), check_vma=False)
```

time: 462 us -> 127 us (0.27)
  local copies, waits for them, and re-layouts: 321 us -> 4.88 us
  Pallas kernels: 0 us -> 104 us
  waiting for transfers between devices: 84 us -> 0 us
  blocking collectives: 13.5 us -> 0 us
  other arithmetic: 28.4 us -> 16.3 us
  starting transfers between devices: 11.5 us -> 0 us
    gather x19 -> x0, local copies, waits for them, and re-layouts: 320 us -> none  [the longest x2 90.6 us: local_part(): sort_order[src_pos]]
    pallas_call x0 -> x3, Pallas kernels: none -> 104 us  [the longest x1 65.4 us: local_part(): pl.pallas_call(functools.partial(exchange_kernel, group, cap, relay, 16),...]
    all_to_all x2 -> x0, waiting for transfers between devices: 84 us -> none  [the longest x1 84 us: local_part(): recv_rows = lax.all_to_all(send_rows, 'g', 0, 0, tiled=True)]
    unnamed x1 -> x0, blocking collectives: 13.5 us -> none
    all_to_all x2 -> x0, starting transfers between devices: 11.5 us -> none  [the longest x1 6.25 us: local_part(): recv_keys = lax.all_to_all(send_keys, 'g', 0, 0, tiled=True)]
    select_n x30 -> x0, other arithmetic: 9.18 us -> none  [the longest x1 8.01 us: local_part(): jnp.where(is_valid[:, :, None], rows_loc[sort_order[src_pos]], 0.0)]
    sort x3 -> x2, other arithmetic: 18 us -> 16.3 us  [the longest x1 9.13 us: local_part(): lax.sort((windows.reshape(-1), locs.reshape(-1)), num_keys=1)]
  transfers between devices with their start and end apart: 2 -> 0, of which waited for: 1 -> 0; matrix products, arithmetic and copies ran while one was open for 37% -> 0% of each run, Pallas kernels for 0% -> 0%
where the time goes in v2:
time: 127 us; the launch traced here: 126 us
  Pallas kernels  104 us (82%)
  other arithmetic  16.3 us (13%)
  local copies, waits for them, and re-layouts  4.88 us (4%)
  between operations  1.4 us (1%)
    pallas_call x1, Pallas kernels, local_part(): pl.pallas_call(functools.partial(exchange_kernel, group, cap, relay, 16),...  65.4 us
    pallas_call x1, Pallas kernels, placed(): pl.pallas_call(functools.partial(place_kernel, block, 32), grid_spec=pltp...  24 us
    pallas_call x1, Pallas kernels, local_part(): pl.pallas_call(functools.partial(plan_kernel, group, n, cap, relay), out_...  14.2 us
    sort x1, other arithmetic, local_part(): lax.sort((windows.reshape(-1), locs.reshape(-1)), num_keys=1)  9.13 us
    sort x1, other arithmetic, local_part(): lax.sort((keys_loc, lax.iota(jnp.int32, n)), num_keys=1)  7.14 us
    unnamed x4, local copies, waits for them, and re-layouts  4.19 us

profile of v2, /device:TPU:113, one launch (start us, length us, event | category | flops | bytes accessed | tf_op | source)
XLA Modules:
  0.0 126.2 jit_solution(14785915279034686212)
XLA Ops:
  0.6 7.1 %sort.53 = (f32[8192]{0:T(1024)S(1)}, s32[8192]{0:T(1024)S(1)}) sort(f32[8192]{0:T(1024)} %param.4, s32[8192]{0:T(1024)S(1)} %iota.13), dimensions={0}, to_apply=%region_0.0 | sort | flops 106496 | bytes 131072 | tf_op jit(solution)/shard_map/sort | solution.py:237
  7.8 14.2 %plan.1 = (f32[128,128]{1,0:T(8,128)S(1)}, s32[128,128]{1,0:T(8,128)S(1)}, bf16[8192,2,128]{2,1,0:T(2,128)(2,1)S(1)}, s32[5,8,128]{2,1,0:T(8,128)S(1)}, s32[8,12...) custom-call(f32[64,128]{1,0:T(8,128)S(1)} %bitcast.29, bf16[8192,256]{1,0:T(8,128)(2,1)} %rows_ref.1), custom_call_target="tpu_custom_call" | custom-call | tf_op jit(solution)/shard_map/plan/pallas_call | solution.py:238
  22.0 0.0 copy-start
  22.1 2.0 %copy-done = bf16[8192,2,128]{2,1,0:T(2,128)(2,1)} copy-done((bf16[8192,2,128]{2,1,0:T(2,128)(2,1)}, bf16[8192,2,128]{2,1,0:T(2,128)(2,1)S(1)}, u32[]{:S(2)}) %copy-start) | copy-done | bytes 4194328
  24.1 9.1 %sort.54 = (f32[16384]{0:T(1024)}, s32[16384]{0:T(1024)S(1)}, s32[16384]{0:T(1024)}) sort(f32[16384]{0:T(1024)S(1)} %bitcast.31, s32[16384]{0:T(1024)S(1)} %bitcast.28, s32[16384]{0:T(1024)S(1)} %iota.14), dimensions={0}, to_apply=%region_1.0 | sort | flops 229376 | bytes 393216 | tf_op jit(solution)/shard_map/sort | solution.py:262
  33.2 0.7 fusion.3
  34.6 0.0 copy-start.1
  34.6 2.2 %copy-done.1 = bf16[8192,2,128]{2,1,0:T(2,128)(2,1)S(1)} copy-done((bf16[8192,2,128]{2,1,0:T(2,128)(2,1)S(1)}, bf16[8192,2,128]{2,1,0:T(2,128)(2,1)}, u32[]{:S(2)}) %copy-start.1) | copy-done | bytes 4194328
  36.8 65.4 %exchange.1 = bf16[9344,2,128]{2,1,0:T(2,128)(2,1)} custom-call(s32[10240]{0:T(1024)S(1)} %concatenate.41.order_ref, s32[128]{0:T(128)S(1)} %dynamic-slice_bitcast_fusion.start_ref, s32[8,128]{1,0:T(8,128)S(1)} %get-tuple-element.52.idx1_ref, s32[8,128]{1,0:T(8,128)S(1)} %get-tuple-element.53.idx2_ref, bf16[8192,2,128]{2,1,0:T(2,128)(2,1)S(1)} %copy-done.1), custom_call_target="tpu_custom_call" | custom-call | tf_op jit(solution)/shard_map/exchange/pallas_call | solution.py:265
  102.2 24.0 %conditional.1 = (bf16[16384,256]{1,0:T(8,128)(2,1)}) conditional(s32[]{:T(128)} %bitcast.24, (s32[2]{0:T(128)S(1)}, s32[128]{0:T(128)S(1)}, s32[10240]{0:T(1024)S(1)}, bf16[8192,256]{1,0:T(8,128)(2,1)}, f32[128,128]{1,0:T(8,128)S(1)}) %tuple.15, (s32[16384]{0:T(1024)S(1)}, s32[2]{0:T(128)S(1)}, bf16[9344,2,128]{2,1,0:T(2,128)(2,1)}) %tuple.16), branch_computations={%region_2.4_spmd, %region_4.5_spmd} | conditional | flops 4571160 | bytes 76644760 | solution.py:309
  102.2 24.0 %place.1 = bf16[16384,256]{1,0:T(8,128)(2,1)} custom-call(s32[16384]{0:T(1024)S(1)} %get-tuple-element.27.loc_ref, s32[2]{0:T(128)S(1)} %get-tuple-element.28.info_ref, bf16[9344,2,128]{2,1,0:T(2,128)(2,1)} %get-tuple-element.29.rows_ref), custom_call_target="tpu_custom_call" | custom-call | tf_op jit(solution)/shard_map/cond/branch_1_fun/place/pallas_call | solution.py:286
  (5 shorter events, 0.0 us)
Async XLA Ops:
  22.0 2.0 %copy-start = (bf16[8192,2,128]{2,1,0:T(2,128)(2,1)}, bf16[8192,2,128]{2,1,0:T(2,128)(2,1)S(1)}, u32[]{:S(2)}) copy-start(bf16[8192,2,128]{2,1,0:T(2,128)(2,1)S(1)} %get-tuple-element.54.rows_ref) | copy-start | bytes 12582916
  34.6 2.2 %copy-start.1 = (bf16[8192,2,128]{2,1,0:T(2,128)(2,1)S(1)}, bf16[8192,2,128]{2,1,0:T(2,128)(2,1)}, u32[]{:S(2)}) copy-start(bf16[8192,2,128]{2,1,0:T(2,128)(2,1)} %copy-done) | copy-start | bytes 12582916

commit v3 on v0

v3 whole, which is shorter than its diff:
```python
import functools

import jax
import jax.numpy as jnp
from jax import lax
from jax.experimental import pallas as pl
from jax.experimental.pallas import tpu as pltpu
from jax.sharding import PartitionSpec as P

PAD_KEY = 128.0
LANES = 128
MESH = pl.DeviceIdType.MESH


def lane_prefix(x, lane):
    for step in (1, 2, 4):
        x = x + jnp.where(lane >= step, pltpu.roll(x, step, 1), 0)
    return x


def sub_prefix(x, sub):
    for step in (1, 2, 4):
        x = x + jnp.where(sub >= step, pltpu.roll(x, step, 0), 0)
    return x


def merge_runs(keys, locs, run_vregs):
    num = len(keys)
    sub = lax.broadcasted_iota(jnp.int32, keys[0].shape, 0)
    lane = lax.broadcasted_iota(jnp.int32, keys[0].shape, 1)
    size = 2 * run_vregs
    while size <= num:
        dist = size // 2
        while dist:
            for v in range(num):
                if v & dist:
                    continue
                a, b = (v, v + dist) if not v & size else (v + dist, v)
                swap = keys[b] < keys[a]
                keys[a], keys[b] = jnp.where(swap, keys[b], keys[a]), jnp.where(swap, keys[a], keys[b])
                locs[a], locs[b] = jnp.where(swap, locs[b], locs[a]), jnp.where(swap, locs[a], locs[b])
            dist //= 2
        for axis, index, extent, steps in ((0, sub, 8, (4, 2, 1)), (1, lane, LANES, (64, 32, 16, 8, 4, 2, 1))):
            for step in steps:
                bit = jnp.bitwise_and(index, step) != 0
                for v in range(num):
                    up = bit if not v & size else jnp.logical_not(bit)

                    def other(x):
                        return jnp.where(bit, pltpu.roll(x, step, axis), pltpu.roll(x, extent - step, axis))

                    peer_key, peer_loc = other(keys[v]), other(locs[v])
                    take = jnp.logical_xor(peer_key < keys[v], up)
                    keys[v] = jnp.where(take, peer_key, keys[v])
                    locs[v] = jnp.where(take, peer_loc, locs[v])
        size *= 2
    return keys, locs


def exchange_kernel(group, n, cap, relay, unroll, keys_ref, order_ref, rows_ref,
                    out_ref, mkey_ref, mloc_ref, win_ref, start_ref, info_ref,
                    all_keys, rows3, near, far1, far2, got, tab_ref, idx1_ref, idx2_ref,
                    tab, order, idx1_sm, idx2_sm,
                    key_sems, near_sems, far1_sems, far2_sems, local_sems):
    run_rows = n // LANES
    win_rows = 2 * run_rows // group
    me = lax.axis_index("g")
    order_copy = pltpu.make_async_copy(order_ref, order.at[pl.ds(0, n)], local_sems.at[0])
    tail_copy = pltpu.make_async_copy(
        order_ref.at[pl.ds(0, order.shape[0] - n)], order.at[pl.ds(n, order.shape[0] - n)], local_sems.at[1])
    order_copy.start()
    tail_copy.start()
    barrier = pltpu.get_barrier_semaphore()
    for off in range(1, group):
        pl.semaphore_signal(barrier, inc=1, device_id={"g": lax.rem(me + off, group)}, device_id_type=MESH)

    def relayout(t, c):
        at = pl.multiple_of(t * 64, 64)
        rows3[pl.ds(at, 64)] = rows_ref[pl.ds(at, 64)].reshape(64, 2, LANES)
        return c

    lax.fori_loop(0, n // 192, relayout, 0)
    pl.semaphore_wait(barrier, group - 1)

    def send(src, dst, sems, off):
        copy = pltpu.make_async_remote_copy(
            src_ref=src, dst_ref=dst, send_sem=sems.at[0, off], recv_sem=sems.at[1, off],
            device_id={"g": lax.rem(me + off, group)}, device_id_type=MESH)
        copy.start()
        return copy

    copies = [send(keys_ref, all_keys.at[me, pl.ds(0, run_rows)], key_sems, off) for off in range(1, group)]
    all_keys[me, pl.ds(0, run_rows)] = keys_ref[...]
    tail = all_keys.shape[1] - run_rows
    for s in range(group):
        all_keys[s, pl.ds(run_rows, tail)] = jnp.full((tail, LANES), PAD_KEY, jnp.float32)
    lax.fori_loop(n // 192, n // 64, relayout, 0)
    for copy in copies:
        copy.wait()

    count = group * group
    stride = run_rows // group
    col = jnp.concatenate(
        [jnp.concatenate([all_keys[s, pl.ds(m * stride, 1)] for m in range(group)], axis=0) for s in range(group)], axis=0)
    col = jnp.broadcast_to(col[:, 0:1], (count, LANES))
    r_id = lax.broadcasted_iota(jnp.int32, (count, LANES), 0)
    l_id = lax.broadcasted_iota(jnp.int32, (count, LANES), 1)
    row = jnp.sum(jnp.where(r_id == l_id, col, 0.0), axis=0, keepdims=True)
    less = (jnp.broadcast_to(row, (count, LANES)) < col) & (l_id < count)
    rank = jnp.sum(jnp.where(less, 1.0, 0.0), axis=1, keepdims=True)
    want = (group * l_id + group // 2).astype(jnp.float32)
    splitters = jnp.sum(jnp.where(jnp.broadcast_to(rank, (count, LANES)) == want, col, 0.0), axis=0, keepdims=True)

    lane = lax.broadcasted_iota(jnp.int32, (group, LANES), 1)
    sub = lax.broadcasted_iota(jnp.int32, (group, LANES), 0)
    edges = jnp.where(lane < group, 0, n)
    for j in range(1, group):
        part = []
        for s in range(group):
            hit = jnp.where(all_keys[s, pl.ds(0, run_rows)] < splitters[0, j], 1, 0)
            part.append(jnp.sum(hit, axis=0, keepdims=True))
        total = jnp.sum(jnp.concatenate(part, axis=0), axis=1, keepdims=True)
        edges = jnp.where(lane == j, jnp.broadcast_to(total, (group, LANES)), edges)
    counts = jnp.where(lane < group, pltpu.roll(edges, LANES - 1, 1) - edges, 0)
    over = jnp.maximum(counts - cap, 0)
    share = jnp.right_shift(over + (group - 1), group.bit_length() - 1)
    first = lane_prefix(share, lane) - share
    second = sub_prefix(share, sub) - share
    worst = jnp.maximum(jnp.max(first + share), jnp.max(second + share))
    for t, x in enumerate((edges, counts, share, first, second)):
        tab_ref[t] = x
    to_smem = pltpu.make_async_copy(tab_ref, tab, local_sems.at[2])
    to_smem.start()
    order_copy.wait()
    tail_copy.wait()
    to_smem.wait()

    idx1 = jnp.zeros((group, LANES), jnp.int32)
    for j in range(group):
        q, a = tab[2, me, j], tab[3, me, j]
        src = tab[0, me, j] + cap - a + q * sub + lane
        idx1 = jnp.where((lane >= a) & (lane < a + q), src, idx1)
    idx1_ref[...] = jnp.clip(idx1, 0, n - 1)
    idx1_copy = pltpu.make_async_copy(idx1_ref, idx1_sm, local_sems.at[3])
    idx1_copy.start()

    def gather(dst, base, size, pick):
        def step(t, c):
            for u in range(unroll):
                dst[base + t * unroll + u] = pick(t * unroll, u)
            return c
        lax.fori_loop(0, size // unroll, step, 0)

    waits, firsts = [], []

    def direct(off):
        start = tab[0, me, lax.rem(me + off, group)]

        def pick(at, u):
            return rows3[order[(start + at) + u]]

        if off:
            gather(near.at[off], 0, cap, pick)
            waits.append(send(near.at[off], out_ref.at[pl.ds(me * cap, cap)], near_sems, off))
        else:
            gather(out_ref, me * cap, cap, pick)

    offsets = [2, 6, 4, 3, 7, 5, 1, 0]
    for off in offsets[:3]:
        direct(off)
    idx1_copy.wait()
    for off in offsets:
        peer = lax.rem(me + off, group)

        def pick(at, u):
            return rows3[order[idx1_sm[peer, at + u]]]

        if off:
            gather(far1.at[off], 0, relay, pick)
            firsts.append(send(far1.at[off], got.at[pl.ds(me * relay, relay)], far1_sems, off))
        else:
            gather(got, me * relay, relay, pick)
    for off in offsets[3:]:
        direct(off)

    lane1 = lane[0:1]
    for j in range(group):
        line = jnp.zeros((1, LANES), jnp.int32)
        for s in range(group):
            q, a, b = tab[2, s, j], tab[3, s, j], tab[4, s, j]
            line = jnp.where((lane1 >= b) & (lane1 < b + q), s * relay + a - b + lane1, line)
        idx2_ref[pl.ds(j, 1)] = jnp.clip(line, 0, group * relay - 1)
    idx2_copy = pltpu.make_async_copy(idx2_ref, idx2_sm, local_sems.at[4])
    idx2_copy.start()

    wl = lax.broadcasted_iota(jnp.int32, (win_rows, LANES), 1)
    pos = lax.broadcasted_iota(jnp.int32, (win_rows, LANES), 0) * LANES + wl
    own = jnp.int32(0)
    run_keys, run_locs = [], []
    for s in range(group):
        start, num = tab[0, s, me], tab[1, s, me]
        q, b = tab[2, s, me], tab[4, s, me]
        own = own + num
        shift = jnp.bitwise_and(start, LANES - 1)
        at = jnp.right_shift(start, LANES.bit_length() - 1)
        turn = jnp.bitwise_and(LANES - shift, LANES - 1)
        one = pltpu.roll(all_keys[s, pl.ds(at, win_rows)], turn, 1)
        two = pltpu.roll(all_keys[s, pl.ds(at + 1, win_rows)], turn, 1)
        window = jnp.where(pos < num, jnp.where(wl < LANES - shift, one, two), PAD_KEY)
        win_ref[pl.ds(s * win_rows, win_rows)] = window
        where = pos
        if s % 2:
            window = jnp.take_along_axis(window, LANES - 1 - wl, axis=1)
            window = jnp.concatenate([window[r:r + 1] for r in range(win_rows - 1, -1, -1)], axis=0)
            where = win_rows * LANES - 1 - pos
        extra = where - cap
        far = group * cap + b + extra
        for m in range(1, group):
            far = far + jnp.where(extra >= m * q, relay - q, 0)
        loc = jnp.where(where < cap, s * cap + where, far)
        loc = jnp.where(where < num, jnp.clip(loc, 0, group * (cap + relay) - 1), 0)
        for v in range(win_rows // 8):
            run_keys.append(window[v * 8:v * 8 + 8])
            run_locs.append(loc[v * 8:v * 8 + 8])
    info_ref[0] = own
    info_ref[1] = jnp.where(worst <= relay, 0, 1)
    for j in range(group):
        start_ref[j] = tab[0, me, j]
    merged, placed = merge_runs(run_keys, run_locs, win_rows // 8)
    for v in range(2 * run_rows // 8):
        mkey_ref[pl.ds(v * 8, 8)] = merged[v]
        mloc_ref[pl.ds(v * 8, 8)] = placed[v]

    idx2_copy.wait()
    for copy in firsts:
        copy.wait()
    base2 = group * cap + me * relay
    for off in offsets:
        peer = lax.rem(me + off, group)

        def pick(at, u):
            return got[idx2_sm[peer, at + u]]

        if off:
            gather(far2.at[off], 0, relay, pick)
            waits.append(send(far2.at[off], out_ref.at[pl.ds(base2, relay)], far2_sems, off))
        else:
            gather(out_ref, base2, relay, pick)
    for copy in waits:
        copy.wait()


def place_kernel(block, chunk, loc_ref, info_ref, rows_ref, out_ref, tmp_a, tmp_b):
    base = pl.program_id(0) * block
    num = jnp.clip(info_ref[0] - base, 0, block)
    width = out_ref.shape[1]

    def fetch(c, tmp):
        at = base + c * chunk
        for u in range(chunk):
            tmp[u] = rows_ref[loc_ref[at + u]]

    def finish(c, tmp):
        at = pl.multiple_of(c * chunk, chunk)
        out_ref[pl.ds(at, chunk)] = tmp[...].reshape(chunk, width)

    pairs = (num + 2 * chunk - 1) // (2 * chunk)

    @pl.when(pairs > 0)
    def _():
        fetch(0, tmp_a)

        def step(t, c):
            fetch(2 * t + 1, tmp_b)
            finish(2 * t, tmp_a)
            fetch(jnp.minimum(2 * t + 2, block // chunk - 1), tmp_a)
            finish(2 * t + 1, tmp_b)
            return c

        lax.fori_loop(0, pairs, step, 0)
        edge = jnp.minimum(num // chunk, block // chunk - 1)
        at = pl.multiple_of(edge * chunk, chunk)
        row = at + lax.broadcasted_iota(jnp.int32, (chunk, width), 0)
        x = out_ref[pl.ds(at, chunk)]
        out_ref[pl.ds(at, chunk)] = jnp.where(row < num, x, jnp.zeros_like(x))

    def blank(t, c):
        at = pl.multiple_of(t * chunk, chunk)
        out_ref[pl.ds(at, chunk)] = jnp.zeros((chunk, width), out_ref.dtype)
        return c

    lax.fori_loop((num + chunk - 1) // chunk, block // chunk, blank, 0)


def solution(mesh):
    group = mesh.shape["g"]

    def local_part(keys_loc, rows_loc):
        n = keys_loc.shape[0]
        width = rows_loc.shape[1]
        full_cap = 2 * n // group
        cap = n // group + n // group // 64
        relay = LANES
        total = group * (cap + relay)
        spec = lambda m: pl.BlockSpec(memory_space=m)
        vmem, smem = pltpu.VMEM, pltpu.SMEM
        dtype = rows_loc.dtype
        run_rows = n // LANES
        pad = -(-cap // LANES) * LANES

        sorted_keys, order = lax.sort((keys_loc, lax.iota(jnp.int32, n)), num_keys=1)
        recv, merged_keys, merged_loc, windows, my_starts, info = pl.pallas_call(
            functools.partial(exchange_kernel, group, n, cap, relay, 16),
            out_shape=[
                jax.ShapeDtypeStruct((total, 2, LANES), dtype),
                jax.ShapeDtypeStruct((2 * run_rows, LANES), jnp.float32),
                jax.ShapeDtypeStruct((2 * run_rows, LANES), jnp.int32),
                jax.ShapeDtypeStruct((2 * run_rows, LANES), jnp.float32),
                jax.ShapeDtypeStruct((group,), jnp.int32),
                jax.ShapeDtypeStruct((2,), jnp.int32),
            ],
            in_specs=[spec(vmem), spec(pl.ANY), spec(vmem)],
            out_specs=[spec(vmem)] * 4 + [spec(smem)] * 2,
            scratch_shapes=[
                pltpu.VMEM((group, run_rows + 24, LANES), jnp.float32),
                pltpu.VMEM((n, 2, LANES), dtype),
                pltpu.VMEM((group, cap, 2, LANES), dtype),
                pltpu.VMEM((group, relay, 2, LANES), dtype),
                pltpu.VMEM((group, relay, 2, LANES), dtype),
                pltpu.VMEM((group * relay, 2, LANES), dtype),
                pltpu.VMEM((5, group, LANES), jnp.int32),
                pltpu.VMEM((group, LANES), jnp.int32),
                pltpu.VMEM((group, LANES), jnp.int32),
                pltpu.SMEM((5, group, LANES), jnp.int32),
                pltpu.SMEM((n + pad,), jnp.int32),
                pltpu.SMEM((group, LANES), jnp.int32),
                pltpu.SMEM((group, LANES), jnp.int32),
            ] + [pltpu.SemaphoreType.DMA((2, group))] * 4 + [pltpu.SemaphoreType.DMA((5,))],
            compiler_params=pltpu.CompilerParams(collective_id=0, has_side_effects=True, vmem_limit_bytes=32 << 20),
            name="exchange",
        )(sorted_keys.reshape(run_rows, LANES), order, rows_loc)

        block = 2048
        chunk = 64
        merged_rows = pl.pallas_call(
            functools.partial(place_kernel, block, chunk),
            grid_spec=pltpu.PrefetchScalarGridSpec(
                num_scalar_prefetch=2,
                grid=(2 * n // block,),
                in_specs=[spec(vmem)],
                out_specs=pl.BlockSpec((block, width), lambda i, *_: (i, 0)),
                scratch_shapes=[pltpu.VMEM((chunk, 2, LANES), dtype)] * 2,
            ),
            out_shape=jax.ShapeDtypeStruct((2 * n, width), dtype),
            compiler_params=pltpu.CompilerParams(vmem_limit_bytes=24 << 20),
            name="place",
        )(merged_loc.reshape(-1), info, recv)

        merged_rows, windows, my_starts, info = lax.optimization_barrier((merged_rows, windows, my_starts, info))

        def padded(carry):
            left, _ = carry
            order_pad = jnp.concatenate([order, jnp.zeros((full_cap,), jnp.int32)])
            at = my_starts + (left - 1)
            send_idx = jnp.concatenate([lax.dynamic_slice(order_pad, (at[d],), (full_cap,)) for d in range(group)])
            send_rows = rows_loc[send_idx].reshape(group, full_cap, width)
            recv_rows = lax.all_to_all(send_rows, "g", 0, 0, tiled=True)
            slots = lax.iota(jnp.int32, 2 * n)
            _, merge_order = lax.sort((windows.reshape(-1), slots), num_keys=1)
            rows = recv_rows.reshape(-1, width)[merge_order]
            return left - 1, jnp.where((slots < info[0])[:, None], rows, 0.0)

        _, merged_rows = lax.while_loop(lambda carry: carry[0] > 0, padded, (info[1], merged_rows))
        return merged_keys.reshape(-1), merged_rows, info[0:1]

    row_spec = P(("batch", "g"))
    mat_spec = P(("batch", "g"), None)
    return jax.shard_map(local_part, mesh=mesh, in_specs=(row_spec, mat_spec), out_specs=(row_spec, mat_spec, row_spec), check_vma=False)
```

time: 462 us -> 99.3 us (0.21)
  local copies, waits for them, and re-layouts: 321 us -> 1.19 us
  Pallas kernels: 0 us -> 89.3 us
  waiting for transfers between devices: 84 us -> 0 us
  other arithmetic: 28.4 us -> 7.14 us
  blocking collectives: 13.5 us -> 0 us
  starting transfers between devices: 11.5 us -> 0 us
    gather x19 -> x0, local copies, waits for them, and re-layouts: 320 us -> none  [the longest x2 90.6 us: local_part(): sort_order[src_pos]]
    pallas_call x0 -> x2, Pallas kernels: none -> 89.3 us  [the longest x1 75.5 us: local_part(): pl.pallas_call(functools.partial(exchange_kernel, group, n, cap, relay, 1...]
    all_to_all x2 -> x0, waiting for transfers between devices: 84 us -> none  [the longest x1 84 us: local_part(): recv_rows = lax.all_to_all(send_rows, 'g', 0, 0, tiled=True)]
    unnamed x1 -> x0, blocking collectives: 13.5 us -> none
    all_to_all x2 -> x0, starting transfers between devices: 11.5 us -> none  [the longest x1 6.25 us: local_part(): recv_keys = lax.all_to_all(send_keys, 'g', 0, 0, tiled=True)]
    sort x3 -> x1, other arithmetic: 18 us -> 7.14 us  [local_part(): lax.sort((keys_loc, lax.iota(jnp.int32, n)), num_keys=1)]
    select_n x30 -> x0, other arithmetic: 9.18 us -> none  [the longest x1 8.01 us: local_part(): jnp.where(is_valid[:, :, None], rows_loc[sort_order[src_pos]], 0.0)]
  transfers between devices with their start and end apart: 2 -> 0, of which waited for: 1 -> 0; matrix products, arithmetic and copies ran while one was open for 37% -> 0% of each run, Pallas kernels for 0% -> 0%
where the time goes in v3:
time: 99.3 us; the launch traced here: 99.1 us
  Pallas kernels  89.3 us (90%)
  other arithmetic  7.14 us (7%)
  local copies, waits for them, and re-layouts  1.19 us (1%)
    pallas_call x1, Pallas kernels, local_part(): pl.pallas_call(functools.partial(exchange_kernel, group, n, cap, relay, 1...  75.5 us
    pallas_call x1, Pallas kernels, local_part(): pl.pallas_call(functools.partial(place_kernel, block, chunk), grid_spec=p...  13.8 us
    sort x1, other arithmetic, local_part(): lax.sort((keys_loc, lax.iota(jnp.int32, n)), num_keys=1)  7.14 us

profile of v3, /device:TPU:113, one launch (start us, length us, event | category | flops | bytes accessed | tf_op | source)
XLA Modules:
  0.0 99.1 jit_solution(4032975809266609885)
XLA Ops:
  0.6 7.1 %sort.36 = (f32[8192]{0:T(1024)S(1)}, s32[8192]{0:T(1024)S(1)}) sort(f32[8192]{0:T(1024)} %param.4, s32[8192]{0:T(1024)S(1)} %iota.16), dimensions={0}, to_apply=%region_0.0 | sort | flops 106496 | bytes 131072 | tf_op jit(solution)/shard_map/sort | solution.py:311
  7.8 75.5 %exchange.1 = (bf16[9344,2,128]{2,1,0:T(2,128)(2,1)S(1)}, f32[128,128]{1,0:T(8,128)S(1)}, s32[128,128]{1,0:T(8,128)S(1)}, f32[128,128]{1,0:T(8,128)S(1)}, s32[8]{0:T(128)S(1)}, /*index=5*/s32[2]{0:T(128)S(1)}) custom-call(f32[64,128]{1,0:T(8,128)S(1)} %bitcast.72, s32[8192]{0:T(1024)S(1)} %get-tuple-element.233.order_ref, bf16[8192,256]{1,0:T(8,128)(2,1)} %rows_ref.1), custom_call_target="tpu_custom_call" | custom-call | tf_op jit(solution)/shard_map/exchange/pallas_call | solution.py:312
  83.3 13.8 %place.1 = bf16[16384,256]{1,0:T(8,128)(2,1)} custom-call(s32[16384]{0:T(1024)S(1)} %bitcast.70, s32[2]{0:T(128)S(1)} %get-tuple-element.232.info_ref, bf16[9344,2,128]{2,1,0:T(2,128)(2,1)S(1)} %get-tuple-element.107.rows_ref), custom_call_target="tpu_custom_call" | custom-call | tf_op jit(solution)/shard_map/place/pallas_call | solution.py:345
  97.1 0.6 fusion.2
  97.7 0.8 while.12
  98.4 0.6 copy.19
  (1 shorter events, 0.0 us)

commit v4 on v3

v4 whole, which is shorter than its diff:
```python
import functools

import jax
import jax.numpy as jnp
from jax import lax
from jax.experimental import pallas as pl
from jax.experimental.pallas import tpu as pltpu
from jax.sharding import PartitionSpec as P

PAD_KEY = 128.0
LANES = 128
MESH = pl.DeviceIdType.MESH


def lane_prefix(x, lane):
    for step in (1, 2, 4):
        x = x + jnp.where(lane >= step, pltpu.roll(x, step, 1), 0)
    return x


def sub_prefix(x, sub):
    for step in (1, 2, 4):
        x = x + jnp.where(sub >= step, pltpu.roll(x, step, 0), 0)
    return x


def merge_runs(keys, locs, run_vregs):
    num = len(keys)
    sub = lax.broadcasted_iota(jnp.int32, keys[0].shape, 0)
    lane = lax.broadcasted_iota(jnp.int32, keys[0].shape, 1)
    size = 2 * run_vregs
    while size <= num:
        dist = size // 2
        while dist:
            for v in range(num):
                if v & dist:
                    continue
                a, b = (v, v + dist) if not v & size else (v + dist, v)
                swap = keys[b] < keys[a]
                keys[a], keys[b] = jnp.where(swap, keys[b], keys[a]), jnp.where(swap, keys[a], keys[b])
                locs[a], locs[b] = jnp.where(swap, locs[b], locs[a]), jnp.where(swap, locs[a], locs[b])
            dist //= 2
        for axis, index, extent, steps in ((0, sub, 8, (4, 2, 1)), (1, lane, LANES, (64, 32, 16, 8, 4, 2, 1))):
            for step in steps:
                bit = jnp.bitwise_and(index, step) != 0
                for v in range(num):
                    up = bit if not v & size else jnp.logical_not(bit)

                    def other(x):
                        return jnp.where(bit, pltpu.roll(x, step, axis), pltpu.roll(x, extent - step, axis))

                    peer_key, peer_loc = other(keys[v]), other(locs[v])
                    take = jnp.logical_xor(peer_key < keys[v], up)
                    keys[v] = jnp.where(take, peer_key, keys[v])
                    locs[v] = jnp.where(take, peer_loc, locs[v])
        size *= 2
    return keys, locs


def exchange_kernel(group, n, cap, relay, pieces, keys_ref, order_ref, rows_hbm,
                    out_ref, mkey_ref, mloc_ref, win_ref, start_ref, own_ref, need_ref,
                    rows_ref, keys_pad, sample, samples, outbox, inbox, rows3, near, far1, far2, got, tab_ref, idx1_ref, idx2_ref,
                    tab, order, idx1_sm, idx2_sm, edge_sm,
                    sample_sems, box_sems, near_sems, half_sems, far1_sems, far2_sems, local_sems, load_sems):
    run_rows = n // LANES
    win_rows = 2 * run_rows // group
    box_rows = win_rows + 8
    me = lax.axis_index("g")
    order_copy = pltpu.make_async_copy(order_ref, order.at[pl.ds(0, n)], local_sems.at[0])
    tail_copy = pltpu.make_async_copy(
        order_ref.at[pl.ds(0, order.shape[0] - n)], order.at[pl.ds(n, order.shape[0] - n)], local_sems.at[1])
    order_copy.start()
    tail_copy.start()
    barrier = pltpu.get_barrier_semaphore()
    for off in range(1, group):
        pl.semaphore_signal(barrier, inc=1, device_id={"g": lax.rem(me + off, group)}, device_id_type=MESH)

    piece = n // pieces
    loads = []
    for p in range(pieces):
        at = pl.ds(p * piece, piece)
        loads.append(pltpu.make_async_copy(rows_hbm.at[at], rows_ref.at[at], load_sems.at[p]))
        loads[p].start()
    stride = run_rows // group
    sample[...] = jnp.concatenate([keys_ref[pl.ds(m * stride, 1)] for m in range(group)], axis=0)
    samples[me] = jnp.concatenate([keys_ref[pl.ds(m * stride, 1)] for m in range(group)], axis=0)
    keys_pad[pl.ds(0, run_rows)] = keys_ref[...]
    tail = keys_pad.shape[0] - run_rows
    keys_pad[pl.ds(run_rows, tail)] = jnp.full((tail, LANES), PAD_KEY, jnp.float32)

    def relayout(t, c):
        at = pl.multiple_of(t * 64, 64)
        rows3[pl.ds(at, 64)] = rows_ref[pl.ds(at, 64)].reshape(64, 2, LANES)
        return c

    def ready(lo, hi):
        for p in range(lo, hi):
            loads[p].wait()
            lax.fori_loop(p * piece // 64, (p + 1) * piece // 64, relayout, 0)

    ready(0, pieces // 2)
    pl.semaphore_wait(barrier, group - 1)

    def send(src, dst, sems, off):
        copy = pltpu.make_async_remote_copy(
            src_ref=src, dst_ref=dst, send_sem=sems.at[0, off], recv_sem=sems.at[1, off],
            device_id={"g": lax.rem(me + off, group)}, device_id_type=MESH)
        copy.start()
        return copy

    offsets = [2, 6, 4, 3, 7, 5, 1, 0]
    copies = [send(sample, samples.at[me], sample_sems, off) for off in offsets[:-1]]
    ready(pieces // 2, pieces)
    for copy in copies:
        copy.wait()

    count = group * group
    col = jnp.broadcast_to(samples[...].reshape(count, LANES)[:, 0:1], (count, LANES))
    r_id = lax.broadcasted_iota(jnp.int32, (count, LANES), 0)
    l_id = lax.broadcasted_iota(jnp.int32, (count, LANES), 1)
    row = jnp.sum(jnp.where(r_id == l_id, col, 0.0), axis=0, keepdims=True)
    less = (jnp.broadcast_to(row, (count, LANES)) < col) & (l_id < count)
    rank = jnp.sum(jnp.where(less, 1.0, 0.0), axis=1, keepdims=True)
    want = (group * l_id + group // 2).astype(jnp.float32)
    splitters = jnp.sum(jnp.where(jnp.broadcast_to(rank, (count, LANES)) == want, col, 0.0), axis=0, keepdims=True)
    below = [jnp.zeros((1, LANES), jnp.int32)]
    for j in range(1, group):
        below.append(jnp.sum(jnp.where(keys_ref[...] < splitters[0, j], 1, 0), axis=0, keepdims=True))
    below = jnp.sum(jnp.concatenate(below, axis=0), axis=1, keepdims=True)
    edges = [jnp.clip(below[j, 0], 0, n) for j in range(group)] + [jnp.int32(n)]

    lane = lax.broadcasted_iota(jnp.int32, (group, LANES), 1)
    sub = lax.broadcasted_iota(jnp.int32, (group, LANES), 0)
    mine = jnp.zeros((8, LANES), jnp.int32)
    for j in range(group):
        edge_sm[j] = edges[j]
        start_ref[j] = edges[j]
        mine = jnp.where(lane == j, edges[j + 1] - edges[j], mine)
    edge_sm[group] = edges[group]
    mine = mine.astype(jnp.float32)
    wl = lax.broadcasted_iota(jnp.int32, (win_rows, LANES), 1)
    pos = lax.broadcasted_iota(jnp.int32, (win_rows, LANES), 0) * LANES + wl
    for off in offsets:
        peer = lax.rem(me + off, group)
        start = edge_sm[peer]
        shift = jnp.bitwise_and(start, LANES - 1)
        at = jnp.clip(jnp.right_shift(start, LANES.bit_length() - 1), 0, run_rows)
        turn = jnp.bitwise_and(LANES - shift, LANES - 1)
        one = pltpu.roll(keys_pad[pl.ds(at, win_rows)], turn, 1)
        two = pltpu.roll(keys_pad[pl.ds(at + 1, win_rows)], turn, 1)
        window = jnp.where(pos < edge_sm[peer + 1] - start, jnp.where(wl < LANES - shift, one, two), PAD_KEY)
        if off:
            outbox[off, pl.ds(0, win_rows)] = window
            outbox[off, pl.ds(win_rows, 8)] = mine
        else:
            inbox[me, pl.ds(0, win_rows)] = window
            inbox[me, pl.ds(win_rows, 8)] = mine
    copies = [send(outbox.at[off], inbox.at[me], box_sems, off) for off in offsets[:-1]]
    order_copy.wait()
    tail_copy.wait()

    def gather(dst, base, size, pick):
        unroll = next(u for u in (40, 32, 16) if size % u == 0)

        def step(t, c):
            for u in range(unroll):
                dst[base + t * unroll + u] = pick(t * unroll, u)
            return c
        lax.fori_loop(0, size // unroll, step, 0)

    waits, firsts = [], []

    def direct(off, low=0, high=cap, sems=near_sems):
        start = edge_sm[lax.rem(me + off, group)] + low

        def pick(at, u):
            return rows3[order[(start + at) + u]]

        size = high - low
        if off:
            gather(near.at[off], low, size, pick)
            waits.append(send(near.at[off, pl.ds(low, size)], out_ref.at[pl.ds(me * cap + low, size)], sems, off))
        else:
            gather(out_ref, me * cap + low, size, pick)

    early = cap // 80 * 40
    for off in offsets[:2]:
        direct(off, 0, early, half_sems)
    for off in offsets[:2]:
        direct(off, early, cap)
    direct(offsets[2])
    for copy in copies:
        copy.wait()
    counts = jnp.concatenate([inbox[s, pl.ds(win_rows, 1)] for s in range(group)], axis=0).astype(jnp.int32)
    counts = jnp.clip(counts, 0, n)
    over = jnp.maximum(counts - cap, 0)
    share = jnp.right_shift(over + (group - 1), group.bit_length() - 1)
    first = lane_prefix(share, lane) - share
    second = sub_prefix(share, sub) - share
    worst = jnp.maximum(jnp.max(first + share), jnp.max(second + share))
    for t, x in enumerate((counts, share, first, second)):
        tab_ref[t] = x
    to_smem = pltpu.make_async_copy(tab_ref, tab, local_sems.at[2])
    to_smem.start()
    direct(offsets[3])
    to_smem.wait()
    idx1 = jnp.zeros((group, LANES), jnp.int32)
    for j in range(group):
        q, a = tab[1, me, j], tab[2, me, j]
        src = edge_sm[j] + cap - a + q * sub + lane
        idx1 = jnp.where((lane >= a) & (lane < a + q), src, idx1)
    idx1_ref[...] = jnp.clip(idx1, 0, n - 1)
    idx1_copy = pltpu.make_async_copy(idx1_ref, idx1_sm, local_sems.at[3])
    idx1_copy.start()
    direct(offsets[4])
    idx1_copy.wait()
    for off in offsets:
        peer = lax.rem(me + off, group)

        def pick(at, u):
            return rows3[order[idx1_sm[peer, at + u]]]

        if off:
            gather(far1.at[off], 0, relay, pick)
            firsts.append(send(far1.at[off], got.at[pl.ds(me * relay, relay)], far1_sems, off))
        else:
            gather(got, me * relay, relay, pick)
    for off in offsets[5:]:
        direct(off)

    lane1 = lane[0:1]
    for j in range(group):
        line = jnp.zeros((1, LANES), jnp.int32)
        for s in range(group):
            q, a, b = tab[1, s, j], tab[2, s, j], tab[3, s, j]
            line = jnp.where((lane1 >= b) & (lane1 < b + q), s * relay + a - b + lane1, line)
        idx2_ref[pl.ds(j, 1)] = jnp.clip(line, 0, group * relay - 1)
    idx2_copy = pltpu.make_async_copy(idx2_ref, idx2_sm, local_sems.at[4])
    idx2_copy.start()

    own = jnp.int32(0)
    run_keys, run_locs = [], []
    for s in range(group):
        num, q, b = tab[0, s, me], tab[1, s, me], tab[3, s, me]
        own = own + num
        window = inbox[s, pl.ds(0, win_rows)]
        win_ref[pl.ds(s * win_rows, win_rows)] = window
        where = pos
        if s % 2:
            window = jnp.take_along_axis(window, LANES - 1 - wl, axis=1)
            window = jnp.concatenate([window[r:r + 1] for r in range(win_rows - 1, -1, -1)], axis=0)
            where = win_rows * LANES - 1 - pos
        extra = where - cap
        far = group * cap + b + extra
        for m in range(1, group):
            far = far + jnp.where(extra >= m * q, relay - q, 0)
        loc = jnp.where(where < cap, s * cap + where, far)
        loc = jnp.where(where < num, jnp.clip(loc, 0, group * (cap + relay) - 1), 0)
        for v in range(win_rows // 8):
            run_keys.append(window[v * 8:v * 8 + 8])
            run_locs.append(loc[v * 8:v * 8 + 8])
    own_ref[0] = own
    need_ref[0] = jnp.where(worst <= relay, 0, 1)
    merged, placed = merge_runs(run_keys, run_locs, win_rows // 8)
    for v in range(2 * run_rows // 8):
        mkey_ref[pl.ds(v * 8, 8)] = merged[v]
        mloc_ref[pl.ds(v * 8, 8)] = placed[v]

    idx2_copy.wait()
    for copy in firsts:
        copy.wait()
    base2 = group * cap + me * relay
    for off in offsets:
        peer = lax.rem(me + off, group)

        def pick(at, u):
            return got[idx2_sm[peer, at + u]]

        if off:
            gather(far2.at[off], 0, relay, pick)
            waits.append(send(far2.at[off], out_ref.at[pl.ds(base2, relay)], far2_sems, off))
        else:
            gather(out_ref, base2, relay, pick)
    for copy in waits:
        copy.wait()


def place_kernel(block, chunk, loc_ref, own_ref, rows_ref, keys_ref, out_ref, out_own_ref, out_keys_ref,
                 loc, bufs, blanks, tmp_a, tmp_b, loc_sems, out_sems, blank_sems, key_sem):
    blocks = out_ref.shape[0] // block
    width = out_ref.shape[1]
    own = jnp.clip(own_ref[0], 0, out_ref.shape[0])
    out_own_ref[0] = own
    used = (own + block - 1) // block

    def loc_copy(b):
        at = pl.ds(pl.multiple_of(b * block, block), block)
        return pltpu.make_async_copy(loc_ref.at[at], loc.at[at], loc_sems.at[b])

    def out_copy(b, src, sem):
        return pltpu.make_async_copy(src, out_ref.at[pl.ds(pl.multiple_of(b * block, block), block)], sem)

    for b in range(blocks):
        loc_copy(b).start()
    keys_copy = pltpu.make_async_copy(keys_ref, out_keys_ref, key_sem)
    keys_copy.start()
    blanks[...] = jnp.zeros_like(blanks)

    def blank(b, c):
        out_copy(b, blanks, blank_sems.at[b]).start()
        return c

    lax.fori_loop(used, blocks, blank, 0)

    def fetch(base, tmp):
        for u in range(chunk):
            tmp[u] = rows_ref[loc[base + u]]

    def one_block(b, carry):
        slot = lax.rem(b, 2)
        base = b * block
        num = jnp.minimum(own - base, block)
        loc_copy(b).wait()

        @pl.when(b >= 2)
        def _():
            out_copy(b - 2, bufs.at[slot], out_sems.at[slot]).wait()

        def finish(c, tmp):
            bufs[slot, pl.ds(pl.multiple_of(c * chunk, chunk), chunk)] = tmp[...].reshape(chunk, width)

        fetch(base, tmp_a)

        def step(t, c):
            fetch(base + (2 * t + 1) * chunk, tmp_b)
            finish(2 * t, tmp_a)
            fetch(base + jnp.minimum(2 * t + 2, block // chunk - 1) * chunk, tmp_a)
            finish(2 * t + 1, tmp_b)
            return c

        lax.fori_loop(0, (num + 2 * chunk - 1) // (2 * chunk), step, 0)

        @pl.when(num < block)
        def _():
            edge = num // chunk
            at = pl.multiple_of(edge * chunk, chunk)
            row = at + lax.broadcasted_iota(jnp.int32, (chunk, width), 0)
            x = bufs[slot, pl.ds(at, chunk)]
            bufs[slot, pl.ds(at, chunk)] = jnp.where(row < num, x, jnp.zeros_like(x))

            def clear(t, c):
                bufs[slot, pl.ds(pl.multiple_of(t * chunk, chunk), chunk)] = jnp.zeros((chunk, width), bufs.dtype)
                return c

            lax.fori_loop(edge + 1, block // chunk, clear, 0)

        out_copy(b, bufs.at[slot], out_sems.at[slot]).start()
        return carry

    lax.fori_loop(0, used, one_block, 0)
    for back in (2, 1):
        @pl.when(used >= back)
        def _():
            b = used - back
            slot = lax.rem(b, 2)
            out_copy(b, bufs.at[slot], out_sems.at[slot]).wait()

    keys_copy.wait()

    def settle(b, c):
        out_copy(b, blanks, blank_sems.at[b]).wait()
        return c

    lax.fori_loop(used, blocks, settle, 0)

    def skip(b, c):
        loc_copy(b).wait()
        return c

    lax.fori_loop(used, blocks, skip, 0)


def solution(mesh):
    group = mesh.shape["g"]

    def local_part(keys_loc, rows_loc):
        n = keys_loc.shape[0]
        width = rows_loc.shape[1]
        full_cap = 2 * n // group
        cap = n // group + n // group // 64
        relay = LANES
        total = group * (cap + relay)
        spec = lambda m: pl.BlockSpec(memory_space=m)
        vmem, smem = pltpu.VMEM, pltpu.SMEM
        dtype = rows_loc.dtype
        run_rows = n // LANES
        pad = -(-cap // LANES) * LANES

        sorted_keys, order = lax.sort((keys_loc, lax.iota(jnp.int32, n)), num_keys=1)
        recv, merged_keys, merged_loc, windows, my_starts, own, need = pl.pallas_call(
            functools.partial(exchange_kernel, group, n, cap, relay, 8),
            out_shape=[
                jax.ShapeDtypeStruct((total, 2, LANES), dtype),
                jax.ShapeDtypeStruct((2 * run_rows, LANES), jnp.float32),
                jax.ShapeDtypeStruct((2 * run_rows, LANES), jnp.int32),
                jax.ShapeDtypeStruct((2 * run_rows, LANES), jnp.float32),
                jax.ShapeDtypeStruct((group,), jnp.int32),
                jax.ShapeDtypeStruct((1,), jnp.int32),
                jax.ShapeDtypeStruct((1,), jnp.int32),
            ],
            in_specs=[spec(vmem), spec(pl.ANY), spec(pl.ANY)],
            out_specs=[spec(vmem)] * 4 + [spec(smem)] * 3,
            scratch_shapes=[
                pltpu.VMEM((n, width), dtype),
                pltpu.VMEM((run_rows + 24, LANES), jnp.float32),
                pltpu.VMEM((group, LANES), jnp.float32),
                pltpu.VMEM((group, group, LANES), jnp.float32),
                pltpu.VMEM((group, 2 * run_rows // group + 8, LANES), jnp.float32),
                pltpu.VMEM((group, 2 * run_rows // group + 8, LANES), jnp.float32),
                pltpu.VMEM((n, 2, LANES), dtype),
                pltpu.VMEM((group, cap, 2, LANES), dtype),
                pltpu.VMEM((group, relay, 2, LANES), dtype),
                pltpu.VMEM((group, relay, 2, LANES), dtype),
                pltpu.VMEM((group * relay, 2, LANES), dtype),
                pltpu.VMEM((4, group, LANES), jnp.int32),
                pltpu.VMEM((group, LANES), jnp.int32),
                pltpu.VMEM((group, LANES), jnp.int32),
                pltpu.SMEM((4, group, LANES), jnp.int32),
                pltpu.SMEM((n + pad,), jnp.int32),
                pltpu.SMEM((group, LANES), jnp.int32),
                pltpu.SMEM((group, LANES), jnp.int32),
                pltpu.SMEM((group + 1,), jnp.int32),
            ] + [pltpu.SemaphoreType.DMA((2, group))] * 6 + [pltpu.SemaphoreType.DMA((5,)), pltpu.SemaphoreType.DMA((8,))],
            compiler_params=pltpu.CompilerParams(collective_id=0, has_side_effects=True, vmem_limit_bytes=32 << 20),
            name="exchange",
        )(sorted_keys.reshape(run_rows, LANES), order, rows_loc)

        block = 1024
        chunk = 64
        blocks = 2 * n // block
        merged_rows, counts, sorted_out = pl.pallas_call(
            functools.partial(place_kernel, block, chunk),
            out_shape=[
                jax.ShapeDtypeStruct((2 * n, width), dtype),
                jax.ShapeDtypeStruct((1,), jnp.int32),
                jax.ShapeDtypeStruct((2 * run_rows, LANES), jnp.float32),
            ],
            in_specs=[spec(pl.ANY), spec(smem), spec(vmem), spec(vmem)],
            out_specs=[spec(pl.ANY), spec(smem), spec(pl.ANY)],
            scratch_shapes=[
                pltpu.SMEM((2 * n,), jnp.int32),
                pltpu.VMEM((2, block, width), dtype),
                pltpu.VMEM((block, width), dtype),
                pltpu.VMEM((chunk, 2, LANES), dtype),
                pltpu.VMEM((chunk, 2, LANES), dtype),
                pltpu.SemaphoreType.DMA((blocks,)),
                pltpu.SemaphoreType.DMA((2,)),
                pltpu.SemaphoreType.DMA((blocks,)),
                pltpu.SemaphoreType.DMA,
            ],
            compiler_params=pltpu.CompilerParams(vmem_limit_bytes=16 << 20),
            name="place",
        )(merged_loc.reshape(-1), own, recv, merged_keys)

        merged_rows, windows, my_starts, need = lax.optimization_barrier((merged_rows, windows, my_starts, need))

        def padded(carry):
            left, _ = carry
            order_pad = jnp.concatenate([order, jnp.zeros((full_cap,), jnp.int32)])
            at = my_starts + (left - 1)
            send_idx = jnp.concatenate([lax.dynamic_slice(order_pad, (at[d],), (full_cap,)) for d in range(group)])
            send_rows = rows_loc[send_idx].reshape(group, full_cap, width)
            recv_rows = lax.all_to_all(send_rows, "g", 0, 0, tiled=True)
            slots = lax.iota(jnp.int32, 2 * n)
            _, merge_order = lax.sort((windows.reshape(-1), slots), num_keys=1)
            rows = recv_rows.reshape(-1, width)[merge_order]
            return left - 1, jnp.where((slots < counts[0])[:, None], rows, 0.0)

        _, merged_rows = lax.while_loop(lambda carry: carry[0] > 0, padded, (need.reshape(()), merged_rows))
        return sorted_out.reshape(-1), merged_rows, counts

    row_spec = P(("batch", "g"))
    mat_spec = P(("batch", "g"), None)
    return jax.shard_map(local_part, mesh=mesh, in_specs=(row_spec, mat_spec), out_specs=(row_spec, mat_spec, row_spec), check_vma=False)
```

time: 99.3 us -> 92.6 us (0.933)
  Pallas kernels: 89.3 us -> 83.1 us
  local copies, waits for them, and re-layouts: 1.19 us -> 0.01 us
    pallas_call x2, Pallas kernels: 89.3 us -> 83.1 us  [the longest x1 70.7 us: local_part(): pl.pallas_call(functools.partial(exchange_kernel, group, n, cap, relay, 8...]
where the time goes in v4:
time: 92.6 us; the launch traced here: 91.8 us
  Pallas kernels  83.1 us (90%)
  other arithmetic  7.14 us (8%)
    pallas_call x1, Pallas kernels, local_part(): pl.pallas_call(functools.partial(exchange_kernel, group, n, cap, relay, 8...  70.7 us
    pallas_call x1, Pallas kernels, local_part(): pl.pallas_call(functools.partial(place_kernel, block, chunk), out_shape=[...  12.3 us
    sort x1, other arithmetic, local_part(): lax.sort((keys_loc, lax.iota(jnp.int32, n)), num_keys=1)  7.14 us

profile of v4, /device:TPU:113, one launch (start us, length us, event | category | flops | bytes accessed | tf_op | source)
XLA Modules:
  0.0 91.8 jit_solution(17131298944110214851)
XLA Ops:
  0.6 7.1 %sort.36 = (f32[8192]{0:T(1024)S(1)}, s32[8192]{0:T(1024)S(1)}) sort(f32[8192]{0:T(1024)} %param.4, s32[8192]{0:T(1024)S(1)} %iota.16), dimensions={0}, to_apply=%region_0.0 | sort | flops 106496 | bytes 131072 | tf_op jit(solution)/shard_map/sort | solution.py:399
  7.8 70.7 %exchange.1 = (bf16[9344,2,128]{2,1,0:T(2,128)(2,1)S(1)}, f32[128,128]{1,0:T(8,128)S(1)}, s32[128,128]{1,0:T(8,128)S(1)}, f32[128,128]{1,0:T(8,128)S(1)}, s32[8]{0:T(128)S(1)}, /*index=5*/s32[1]{0:T(128)}, s32[1]{0:T(128)}) custom-call(f32[64,128]{1,0:T(8,128)S(1)} %bitcast.68, s32[8192]{0:T(1024)S(1)} %get-tuple-element.239.order_ref, ...), custom_call_target="tpu_custom_call" | custom-call | tf_op jit(solution)/shard_map/exchange/pallas_call | solution.py:400
  78.5 12.3 %place.1 = (bf16[16384,256]{1,0:T(8,128)(2,1)}, s32[1]{0:T(128)}, f32[128,128]{1,0:T(8,128)}) custom-call(s32[16384]{0:T(1024)S(1)} %bitcast.67, s32[1]{0:T(128)} %get-tuple-element.109.own_ref, bf16[9344,2,128]{2,1,0:T(2,128)(2,1)S(1)} %get-tuple-element.110.rows_ref, f32[128,128]{1,0:T(8,128)S(1)} %get-tuple-element.111.keys_ref), custom_call_target="tpu_custom_call" | custom-call | tf_op jit(solution)/shard_map/place/pallas_call | solution.py:441
  90.9 0.7 while.12
  (1 shorter events, 0.0 us)

commit v5 on v4

--- a/solution.py
+++ b/solution.py
@@ -98,7 +98,7 @@
             loads[p].wait()
             lax.fori_loop(p * piece // 64, (p + 1) * piece // 64, relayout, 0)
 
-    ready(0, pieces // 2)
+    ready(0, pieces // 4)
     pl.semaphore_wait(barrier, group - 1)
 
     def send(src, dst, sems, off):
@@ -110,7 +110,7 @@
 
     offsets = [2, 6, 4, 3, 7, 5, 1, 0]
     copies = [send(sample, samples.at[me], sample_sems, off) for off in offsets[:-1]]
-    ready(pieces // 2, pieces)
+    ready(pieces // 4, pieces)
     for copy in copies:
         copy.wait()
 
@@ -138,6 +138,36 @@
         mine = jnp.where(lane == j, edges[j + 1] - edges[j], mine)
     edge_sm[group] = edges[group]
     mine = mine.astype(jnp.float32)
+    order_copy.wait()
+    tail_copy.wait()
+
+    def gather(dst, base, size, pick):
+        unroll = next(u for u in (43, 40, 32, 16) if size % u == 0)
+
+        def step(t, c):
+            for u in range(unroll):
+                dst[base + t * unroll + u] = pick(t * unroll, u)
+            return c
+        lax.fori_loop(0, size // unroll, step, 0)
+
+    waits, firsts = [], []
+
+    def direct(off, low=0, high=cap, sems=near_sems):
+        start = edge_sm[lax.rem(me + off, group)] + low
+
+        def pick(at, u):
+            return rows3[order[(start + at) + u]]
+
+        size = high - low
+        if off:
+            gather(near.at[off], low, size, pick)
+            waits.append(send(near.at[off, pl.ds(low, size)], out_ref.at[pl.ds(me * cap + low, size)], sems, off))
+        else:
+            gather(out_ref, me * cap + low, size, pick)
+
+    early = cap // 86 * 43
+    for off in offsets[:2]:
+        direct(off, 0, early, half_sems)
     wl = lax.broadcasted_iota(jnp.int32, (win_rows, LANES), 1)
     pos = lax.broadcasted_iota(jnp.int32, (win_rows, LANES), 0) * LANES + wl
     for off in offsets:
@@ -156,39 +186,8 @@
             inbox[me, pl.ds(0, win_rows)] = window
             inbox[me, pl.ds(win_rows, 8)] = mine
     copies = [send(outbox.at[off], inbox.at[me], box_sems, off) for off in offsets[:-1]]
-    order_copy.wait()
-    tail_copy.wait()
-
-    def gather(dst, base, size, pick):
-        unroll = next(u for u in (40, 32, 16) if size % u == 0)
-
-        def step(t, c):
-            for u in range(unroll):
-                dst[base + t * unroll + u] = pick(t * unroll, u)
-            return c
-        lax.fori_loop(0, size // unroll, step, 0)
-
-    waits, firsts = [], []
-
-    def direct(off, low=0, high=cap, sems=near_sems):
-        start = edge_sm[lax.rem(me + off, group)] + low
-
-        def pick(at, u):
-            return rows3[order[(start + at) + u]]
-
-        size = high - low
-        if off:
-            gather(near.at[off], low, size, pick)
-            waits.append(send(near.at[off, pl.ds(low, size)], out_ref.at[pl.ds(me * cap + low, size)], sems, off))
-        else:
-            gather(out_ref, me * cap + low, size, pick)
-
-    early = cap // 80 * 40
-    for off in offsets[:2]:
-        direct(off, 0, early, half_sems)
     for off in offsets[:2]:
         direct(off, early, cap)
-    direct(offsets[2])
     for copy in copies:
         copy.wait()
     counts = jnp.concatenate([inbox[s, pl.ds(win_rows, 1)] for s in range(group)], axis=0).astype(jnp.int32)
@@ -202,7 +201,7 @@
         tab_ref[t] = x
     to_smem = pltpu.make_async_copy(tab_ref, tab, local_sems.at[2])
     to_smem.start()
-    direct(offsets[3])
+    direct(offsets[2])
     to_smem.wait()
     idx1 = jnp.zeros((group, LANES), jnp.int32)
     for j in range(group):
@@ -212,7 +211,6 @@
     idx1_ref[...] = jnp.clip(idx1, 0, n - 1)
     idx1_copy = pltpu.make_async_copy(idx1_ref, idx1_sm, local_sems.at[3])
     idx1_copy.start()
-    direct(offsets[4])
     idx1_copy.wait()
     for off in offsets:
         peer = lax.rem(me + off, group)
@@ -225,7 +223,7 @@
             firsts.append(send(far1.at[off], got.at[pl.ds(me * relay, relay)], far1_sems, off))
         else:
             gather(got, me * relay, relay, pick)
-    for off in offsets[5:]:
+    for off in offsets[3:]:
         direct(off)
 
     lane1 = lane[0:1]
@@ -387,7 +385,7 @@
         n = keys_loc.shape[0]
         width = rows_loc.shape[1]
         full_cap = 2 * n // group
-        cap = n // group + n // group // 64
+        cap = n // group + n // group // 128
         relay = LANES
         total = group * (cap + relay)
         spec = lambda m: pl.BlockSpec(memory_space=m)

time: 92.6 us -> 91.7 us (level)
  no operation moved by 1% of the time
where the time goes in v5:
time: 91.7 us; the launch traced here: 91.5 us
  Pallas kernels  82.8 us (90%)
  other arithmetic  7.14 us (8%)
    pallas_call x1, Pallas kernels, local_part(): pl.pallas_call(functools.partial(exchange_kernel, group, n, cap, relay, 8...  70.5 us
    pallas_call x1, Pallas kernels, local_part(): pl.pallas_call(functools.partial(place_kernel, block, chunk), out_shape=[...  12.3 us
    sort x1, other arithmetic, local_part(): lax.sort((keys_loc, lax.iota(jnp.int32, n)), num_keys=1)  7.14 us

profile of v5, /device:TPU:113, one launch (start us, length us, event | category | flops | bytes accessed | tf_op | source)
XLA Modules:
  0.0 91.5 jit_solution(9633269473027302993)
XLA Ops:
  0.6 7.1 %sort.36 = (f32[8192]{0:T(1024)S(1)}, s32[8192]{0:T(1024)S(1)}) sort(f32[8192]{0:T(1024)} %param.4, s32[8192]{0:T(1024)S(1)} %iota.16), dimensions={0}, to_apply=%region_0.0 | sort | flops 106496 | bytes 131072 | tf_op jit(solution)/shard_map/sort | solution.py:397
  7.8 70.5 %exchange.1 = (bf16[9280,2,128]{2,1,0:T(2,128)(2,1)S(1)}, f32[128,128]{1,0:T(8,128)S(1)}, s32[128,128]{1,0:T(8,128)S(1)}, f32[128,128]{1,0:T(8,128)S(1)}, s32[8]{0:T(128)S(1)}, /*index=5*/s32[1]{0:T(128)}, s32[1]{0:T(128)}) custom-call(f32[64,128]{1,0:T(8,128)S(1)} %bitcast.68, s32[8192]{0:T(1024)S(1)} %get-tuple-element.239.order_ref, ...), custom_call_target="tpu_custom_call" | custom-call | tf_op jit(solution)/shard_map/exchange/pallas_call | solution.py:398
  78.3 12.3 %place.1 = (bf16[16384,256]{1,0:T(8,128)(2,1)}, s32[1]{0:T(128)}, f32[128,128]{1,0:T(8,128)}) custom-call(s32[16384]{0:T(1024)S(1)} %bitcast.67, s32[1]{0:T(128)} %get-tuple-element.109.own_ref, bf16[9280,2,128]{2,1,0:T(2,128)(2,1)S(1)} %get-tuple-element.110.rows_ref, f32[128,128]{1,0:T(8,128)S(1)} %get-tuple-element.111.keys_ref), custom_call_target="tpu_custom_call" | custom-call | tf_op jit(solution)/shard_map/place/pallas_call | solution.py:439
  90.6 0.7 while.12
  (1 shorter events, 0.0 us)

commit v6 on v5

--- a/solution.py
+++ b/solution.py
@@ -433,7 +433,7 @@
             name="exchange",
         )(sorted_keys.reshape(run_rows, LANES), order, rows_loc)
 
-        block = 1024
+        block = 2048
         chunk = 64
         blocks = 2 * n // block
         merged_rows, counts, sorted_out = pl.pallas_call(

time: 91.7 us -> 91.4 us (level)
  no operation moved by 1% of the time
where the time goes in v6:
time: 91.4 us; the launch traced here: 91.2 us
  Pallas kernels  82.5 us (90%)
  other arithmetic  7.14 us (8%)
    pallas_call x1, Pallas kernels, local_part(): pl.pallas_call(functools.partial(exchange_kernel, group, n, cap, relay, 8...  70.5 us
    pallas_call x1, Pallas kernels, local_part(): pl.pallas_call(functools.partial(place_kernel, block, chunk), out_shape=[...  12 us
    sort x1, other arithmetic, local_part(): lax.sort((keys_loc, lax.iota(jnp.int32, n)), num_keys=1)  7.14 us

profile of v6, /device:TPU:113, one launch (start us, length us, event | category | flops | bytes accessed | tf_op | source)
XLA Modules:
  0.0 91.2 jit_solution(5556349165927470634)
XLA Ops:
  0.6 7.1 %sort.36 = (f32[8192]{0:T(1024)S(1)}, s32[8192]{0:T(1024)S(1)}) sort(f32[8192]{0:T(1024)} %param.4, s32[8192]{0:T(1024)S(1)} %iota.16), dimensions={0}, to_apply=%region_0.0 | sort | flops 106496 | bytes 131072 | tf_op jit(solution)/shard_map/sort | solution.py:397
  7.8 70.5 %exchange.1 = (bf16[9280,2,128]{2,1,0:T(2,128)(2,1)S(1)}, f32[128,128]{1,0:T(8,128)S(1)}, s32[128,128]{1,0:T(8,128)S(1)}, f32[128,128]{1,0:T(8,128)S(1)}, s32[8]{0:T(128)S(1)}, /*index=5*/s32[1]{0:T(128)}, s32[1]{0:T(128)}) custom-call(f32[64,128]{1,0:T(8,128)S(1)} %bitcast.68, s32[8192]{0:T(1024)S(1)} %get-tuple-element.239.order_ref, ...), custom_call_target="tpu_custom_call" | custom-call | tf_op jit(solution)/shard_map/exchange/pallas_call | solution.py:398
  78.3 12.0 %place.1 = (bf16[16384,256]{1,0:T(8,128)(2,1)}, s32[1]{0:T(128)}, f32[128,128]{1,0:T(8,128)}) custom-call(s32[16384]{0:T(1024)S(1)} %bitcast.67, s32[1]{0:T(128)} %get-tuple-element.109.own_ref, bf16[9280,2,128]{2,1,0:T(2,128)(2,1)S(1)} %get-tuple-element.110.rows_ref, f32[128,128]{1,0:T(8,128)S(1)} %get-tuple-element.111.keys_ref), custom_call_target="tpu_custom_call" | custom-call | tf_op jit(solution)/shard_map/place/pallas_call | solution.py:439
  90.3 0.7 while.12
  (1 shorter events, 0.0 us)
